TPU v7x, 128 devices: a whole 4x4x4 slice. The times are simulated.
128 devices in a mesh: outer: 16 (over y, x), span: 8 (over z, core).
Axes of the slice: x: 4, y: 4, z: 4, core: 2. Of those that a mesh axis runs over, the one named last changes fastest.
Arguments:
- queries_in: bfloat16 [32, 4096, 16, 128], P('outer', 'span'), may hold values from -6 to 6
- keys_in: bfloat16 [32, 4096, 16, 128], P('outer', 'span'), may hold values from -6 to 6
- values_in: bfloat16 [32, 4096, 16, 128], P('outer', 'span'), may hold values from -6 to 6
- gate_rows: bfloat16 [32, 4096, 16, 128], P('outer', 'span'), may hold values from -6 to 6
- out_weight: bfloat16 [2048, 2048], P('outer'), may hold values from -0.125 to 0.125
Outputs:
- mixer_out: bfloat16 [32, 4096, 2048], P('outer', 'span')
All inputs are finite; a program needn't handle non-finite values.
Results may differ from a plain program's by a relative error of at most 0.0023.
Values may be sent and summed in bfloat16 or wider, within the bound.
A program may use at most 256 MiB of HBM per device.

v0:
```python
import jax
import jax.numpy as jnp
from jax import lax
from jax.sharding import PartitionSpec as P


def taken_in(value, axis, dim, absorb, carry):
    whole = jax.tree.map(lambda part: lax.all_gather(part, axis, axis=dim, tiled=True), value)
    return absorb(carry, whole, jnp.int32(0))


def feature_map(values):
    wide = values.astype(jnp.float32)
    return jnp.where(wide > 0.0, wide + 1.0, jnp.exp(jnp.minimum(wide, 0.0))).astype(jnp.bfloat16)


def close_heads(read, gate_rows, count):
    result = read * count**0.5
    result = result * jax.nn.sigmoid(gate_rows.astype(jnp.float32))
    return result.astype(jnp.bfloat16)


def ask_state(features, state, mass):
    top = jnp.einsum(
        "bthd,bhde->bthe", features, state.astype(jnp.bfloat16), preferred_element_type=jnp.float32
    )
    bottom = jnp.einsum(
        "bthd,bhd->bth", features.astype(jnp.float32), mass, precision=lax.Precision.HIGHEST
    )
    return top / (bottom + 0.001)[..., None]


def body(queries_in, keys_in, values_in, gate_rows, out_weight):
    query_feature, key_feature = (feature_map(queries_in), feature_map(keys_in))
    count = queries_in.shape[1] * lax.axis_size("span")
    part_state = jnp.einsum(
        "bthd,bthe->bhde", key_feature, values_in, preferred_element_type=jnp.float32
    )
    part_mass = jnp.sum(key_feature.astype(jnp.float32), axis=1)
    state, mass = lax.psum((part_state, part_mass), "span")
    read = ask_state(query_feature, state / count, mass / count)
    mixed = close_heads(read, gate_rows, count)
    mixed = mixed.reshape(mixed.shape[0], mixed.shape[1], -1)

    def add_rows(carry, piece, start):
        part = lax.dynamic_slice_in_dim(mixed, start, piece.shape[0], axis=2)
        return carry + jnp.einsum("btw,wv->btv", part, piece, preferred_element_type=jnp.float32)

    blank = jnp.zeros(mixed.shape, jnp.float32)
    mixer_out = taken_in(out_weight, "outer", 0, add_rows, blank).astype(jnp.bfloat16)
    return mixer_out


def solution(mesh):
    in_specs = (
        P("outer", "span", None, None),
        P("outer", "span", None, None),
        P("outer", "span", None, None),
        P("outer", "span", None, None),
        P("outer", None),
    )
    out_specs = P("outer", "span", None)
    return jax.shard_map(body, mesh=mesh, in_specs=in_specs, out_specs=out_specs, check_vma=False)
```

profile of v0, /device:TPU:1, one launch (start us, length us, event | category | flops | bytes accessed | tf_op | source)
XLA Modules:
  0.0 121.4 jit_solution(17295138545519870181)
XLA Ops:
  7.4 0.0 all-reduce.2.cloned.1.call-start
  7.4 7.5 %copy.6 = bf16[2,512,16,128]{1,3,2,0:T(8,128)(2,1)} copy(bf16[2,512,16,128]{3,2,1,0:T(8,128)(2,1)} %param.6) | data formatting | bytes 8388608 | tf_op args[1]
  14.9 7.9 %fusion.11 = f32[2,16,128,128]{2,3,1,0:T(8,128)} fusion(bf16[2,512,16,128]{3,2,1,0:T(8,128)(2,1)} %param.7, bf16[2,512,16,128]{1,3,2,0:T(8,128)(2,1)} %copy.6), kind=kOutput, calls=%fused_computation.19 | convolution fusion | flops 549453824 | bytes 10485760 | tf_op jit(solution)/shard_map/bthd,bthe->bhde/dot_general | solution.py:36
  22.8 0.0 all-reduce.2.cloned.1.call-update
  22.8 0.0 all-gather.2.cloned.1.call-start
  22.9 0.5 all-gather.2.cloned.1.call-update
  23.4 7.5 %copy.7 = bf16[2,512,16,128]{1,3,2,0:T(8,128)(2,1)} copy(bf16[2,512,16,128]{3,2,1,0:T(8,128)(2,1)} %param.5) | data formatting | bytes 8388608 | tf_op args[0]
  30.9 7.5 %copy.9 = bf16[2,512,16,128]{1,3,2,0:T(8,128)(2,1)} copy(bf16[2,512,16,128]{3,2,1,0:T(8,128)(2,1)} %param.8) | data formatting | bytes 8388608 | tf_op args[3]
  38.4 3.9 %convert_reduce_fusion = f32[2,16,128]{2,1,0:T(8,128)S(1)} fusion(bf16[2,512,16,128]{1,3,2,0:T(8,128)(2,1)} %copy.6), kind=kLoop, calls=%fused_computation.18 | loop fusion | flops 16773120 | bytes 4210688 | tf_op jit(solution)/shard_map/reduce_sum | solution.py:39
  42.3 25.3 %psum.15 = f32[2,16,128]{2,1,0:T(8,128)S(1)} all-reduce(f32[2,16,128]{2,1,0:T(8,128)S(1)} %convert_reduce_fusion), channel_id=1, replica_groups=mesh['outer'=16,'span'=8] {'span'}, use_global_device_ids=true, to_apply=%region_2.3 | all-reduce | flops 4096 | bytes 32768 | tf_op jit(solution)/shard_map/psum | solution.py:40
  67.6 5.4 %fusion.17 = f32[2,16,1,512]{3,2,1,0:T(1,128)S(1)} fusion(f32[2,16,128,1]{2,3,1,0:T(1,128)S(1)} %bitcast.25, bf16[2,512,16,128]{1,3,2,0:T(8,128)(2,1)} %copy.7), kind=kOutput, calls=%fused_computation.23 | convolution fusion | flops 37748736 | bytes 4276224 | tf_op jit(solution)/shard_map/bthd,bhd->bth/dot_general | solution.py:27
  73.1 18.1 %all-reduce.2.cloned.1.call-done = f32[2,16,128,128]{2,3,1,0:T(8,128)} async-done(((f32[2,16,128,128]{2,3,1,0:T(8,128)}), f32[2,16,128,128]{2,3,1,0:T(8,128)}) %all-reduce.2.cloned.1.call-update) | async-done | bytes 2097168 | tf_op jit(solution)/shard_map/psum | solution.py:40
  91.2 8.9 %fusion.10 = bf16[2,512,16,128]{1,3,2,0:T(8,128)(2,1)} fusion(bf16[2,512,16,128]{1,3,2,0:T(8,128)(2,1)} %copy.9, f32[2,512,16]{1,2,0:T(8,128)S(1)} %fusion.21, bf16[2,512,16,128]{1,3,2,0:T(8,128)(2,1)} %copy.7, f32[2,16,128,128]{2,3,1,0:T(8,128)} %all-reduce.2.cloned.1.call-done), kind=kOutput, calls=%fused_computation.17 | convolution fusion | flops 567279616 | bytes 14745600 | tf_op jit(solution)/shard_map/bthd,bhde->bthe/dot_general | solution.py:24
  100.0 0.0 all-gather.2.cloned.1.call-done
  100.0 13.9 %fusion.13 = bf16[2,512,2048]{2,1,0:T(8,128)(2,1)} fusion(bf16[2,512,2048]{1,2,0:T(8,128)(2,1)} %bitcast.26, bf16[2048,2048]{1,0:T(8,128)(2,1)} %all-gather.2.cloned.1.call-done), kind=kOutput, calls=%fused_computation.21 | convolution fusion | flops 8592031744 | bytes 16777216 | tf_op jit(solution)/shard_map/btw,wv->btv/dot_general | solution.py:47
  (2 shorter events, 0.0 us)
Async XLA Ops:
  7.4 83.8 %all-reduce.2.cloned.1.call-start = ((), (), s32[]{:S(2)}) async-start(), calls=%async_computation | async-start | bytes 4194304 | tf_op jit(solution)/shard_map/psum | solution.py:40
  22.8 77.2 %all-gather.2.cloned.1.call-start = ((), (), s32[]{:S(2)}) async-start(), calls=%async_computation.1 | async-start | bytes 8912896 | tf_op jit(solution)/shard_map/all_gather | solution.py:8
Sparse Core Ops, SparseCore 0:
  22.9 68.1 all-reduce.1
Sparse Core Ops, SparseCore 1:
  25.4 73.3 all-gather.1
where the time goes:
time: 124 us; the launch traced here: 121 us
  matrix products  36.1 us (29%)
  blocking collectives  25.3 us (20%)
  local copies, waits for them, and re-layouts  22.5 us (18%)
  waiting for transfers between devices  18.6 us (15%)
  between operations  14.9 us (12%)
  other arithmetic  3.92 us (3%)
    psum x1, blocking collectives, body(): state, mass = lax.psum((part_state, part_mass), 'span')  25.3 us
    unnamed x3, local copies, waits for them, and re-layouts  22.5 us
    psum x1, waiting for transfers between devices, body(): state, mass = lax.psum((part_state, part_mass), 'span')  18.1 us
    dot_general x1, matrix products, add_rows(): jnp.einsum('btw,wv->btv', part, piece, preferred_element_type=jnp.float32)  13.9 us
    dot_general x1, matrix products, ask_state(): jnp.einsum('bthd,bhde->bthe', features, state.astype(jnp.bfloat16), prefe...  8.86 us
    dot_general x1, matrix products, body(): jnp.einsum('bthd,bthe->bhde', key_feature, values_in, preferred_element_t...  7.87 us
    dot_general x1, matrix products, ask_state(): jnp.einsum('bthd,bhd->bth', features.astype(jnp.float32), mass, precision...  5.43 us
    reduce_sum x1, other arithmetic, body(): part_mass = jnp.sum(key_feature.astype(jnp.float32), axis=1)  3.91 us
  transfers between devices with their start and end apart: 2, of which 1 were waited for; matrix products, arithmetic and copies ran while one was open for 27% of the time, Pallas kernels for 0%

commit v1 on v0

v1 whole, which is shorter than its diff:
```python
import functools
import jax
import jax.numpy as jnp
from jax import lax
from jax.experimental import pallas as pl
from jax.experimental.pallas import tpu as pltpu
from jax.sharding import PartitionSpec as P

f32 = jnp.float32
bf16 = jnp.bfloat16
MESH = pl.DeviceIdType.MESH

SEQS = 2
T = 512
HEADS = 16
D = 128
WIDTH = HEADS * D
COUNT = 4096
PITCH = T + 4
TC = 64
HG = 4
PIECES = 4
ROWS = 32


def feature(x):
    return jnp.maximum(x, 0.0) + jnp.exp(jnp.minimum(x, 0.0))


def spread(src, dst, seq, fn):
    def step(i, carry):
        start = i * TC
        values = fn(src[seq, pl.ds(start, TC)].astype(f32))
        for t in range(TC):
            for half in range(2):
                dst[pl.ds(start + t + 8 * half * PITCH, 8, stride=PITCH), :] = values[
                    t, 8 * half : 8 * half + 8, :
                ]
        return carry

    lax.fori_loop(0, T // TC, step, 0)


def attention(
    q_in, k_in, v_in, g_in, w_in,
    mixed_out, w_out,
    q_nat, k_nat, v_nat, g_nat,
    fa, fb, factor, q_head, part, mass, mass_in,
    core_in, zs1, zr1, zs2, zr2, state, mixed, w_buf,
    load_sem, w_load_sem, out_sem,
    core_send, core_recv, z_send, z_recv, st_send, st_recv, mass_send, mass_recv,
    ws_sem, wr_sem, wp_sem, wo_sem,
):
    o = lax.axis_index("outer")
    s = lax.axis_index("span")
    core = lax.rem(s, 2)
    z = lax.div(s, 2)
    other = s + 1 - 2 * core
    first = s + 2 * (1 - 2 * lax.rem(z, 2))
    second = 2 * (3 - z) + core
    sa = 1 + 3 * core
    sb = 4 - 3 * core
    a = lax.rem(lax.div(o, sa), 4)
    b = lax.rem(lax.div(o, sb), 4)

    def shard(da, db):
        return lax.rem(a + da, 4) * sa + lax.rem(b + db, 4) * sb

    arrays = (k_in, v_in, q_in, g_in)
    natural = (k_nat, v_nat, q_nat, g_nat)
    step = T // PIECES

    def load(i, seq, piece):
        rows = pl.ds(piece * step, step)
        return pltpu.make_async_copy(
            arrays[i].at[seq, rows], natural[i].at[seq, rows], load_sem.at[i, seq, piece]
        )

    def start_load(i, seq):
        for piece in range(PIECES):
            load(i, seq, piece).start()

    def wait_load(i, seq):
        for piece in range(PIECES):
            load(i, seq, piece).wait()

    start_load(0, 0)
    start_load(1, 0)
    own_w = pltpu.make_async_copy(w_in, w_buf.at[o], w_load_sem)
    own_w.start()
    start_load(0, 1)
    start_load(1, 1)
    for seq in range(SEQS):
        start_load(2, seq)
        start_load(3, seq)

    barrier = pltpu.get_barrier_semaphore()
    for da, db in ((1, 0), (3, 0), (0, 1), (0, 3)):
        pl.semaphore_signal(barrier, inc=1, device_id=(shard(da, db), s), device_id_type=MESH)
    for d in range(1, 8):
        pl.semaphore_signal(barrier, inc=1, device_id=(o, lax.rem(s + d, 8)), device_id_type=MESH)
    pl.semaphore_wait(barrier, 11)

    KINDS = {"A+": (1, 0), "A-": (3, 0), "B+": (0, 1), "B-": (0, 3)}

    def w_copy(kind, da, db, h):
        ref = w_buf.at[shard(da, db), core, h]
        if kind == "P":
            return pltpu.make_async_remote_copy(
                src_ref=ref, dst_ref=ref, send_sem=ws_sem.at[4, da, db, h], recv_sem=wp_sem.at[da, db, h],
                device_id=(o, other), device_id_type=MESH,
            )
        ka, kb = KINDS[kind]
        return pltpu.make_async_remote_copy(
            src_ref=ref,
            dst_ref=ref,
            send_sem=ws_sem.at[list(KINDS).index(kind), da, db, h],
            recv_sem=wr_sem.at[(da - ka) % 4, (db - kb) % 4, h],
            device_id=(shard(ka, kb), s),
            device_id_type=MESH,
        )

    def arrival(ref, sem):
        pltpu.make_async_remote_copy(
            src_ref=ref, dst_ref=ref, send_sem=ws_sem.at[0, 0, 0, 0], recv_sem=sem,
            device_id=(o, other), device_id_type=MESH,
        ).wait_recv()

    sent = []

    def w_send(kind, da, db, h):
        w_copy(kind, da, db, h).start()
        sent.append((kind, da, db, h))

    def w_arrive(da, db, h):
        arrival(w_buf.at[shard(da, db), core, h], wr_sem.at[da, db, h])
        if db == 0:
            if da == 3 and h == 0:
                w_send("A+", da, db, h)
            if da == 1 and h == 1:
                w_send("A-", da, db, h)
            w_send("B+", da, db, h)
            w_send("B-", da, db, h)
        elif db == 3 and h == 0:
            w_send("B+", da, db, h)
        elif db == 1 and h == 1:
            w_send("B-", da, db, h)
        w_send("P", da, db, h)
        w_store(shard(da, db), core, h, da, db, 0).start()

    def w_store(row, c, h, da, db, which):
        return pltpu.make_async_copy(
            w_buf.at[row, c, h], w_out.at[row, c, h], wo_sem.at[which, da, db, h]
        )

    def w_from_partner(da, db, h):
        row = shard(db, da)
        arrival(w_buf.at[row, 1 - core, h], wp_sem.at[da, db, h])
        w_store(row, 1 - core, h, da, db, 1).start()

    groups = []
    for da in (0, 3, 1, 2):
        if da == 0:
            groups.append([(3, 0, 0), (1, 0, 1), (0, 3, 0), (0, 1, 1)])
            groups.append([(3, 0, 1), (1, 0, 0), (0, 3, 1), (0, 1, 0)])
            groups.append([(2, 0, 0), (2, 0, 1), (0, 2, 0), (0, 2, 1)])
        else:
            groups.append([(da, 3, 0), (da, 1, 1)])
            groups.append([(da, 3, 1), (da, 1, 0)])
            groups.append([(da, 2, 0), (da, 2, 1)])

    def service(i):
        for chunk in groups[i]:
            w_arrive(*chunk)

    own_w.wait()
    for kinds, h in ((("A+", "B+"), 0), (("A-", "B-"), 1), (("A+", "B+"), 1), (("A-", "B-"), 0)):
        for kind in kinds:
            w_send(kind, 0, 0, h)
    for c in range(2):
        for h in range(2):
            w_store(o, c, h, 0, 0, c).start()

    mine = core * 8
    theirs = 8 - mine

    def heads(seq, base):
        def group(i, carry):
            for j in range(HG):
                h = base + i * HG + j
                key = fa[pl.ds(h * PITCH, T), :].astype(bf16)
                value = fb[pl.ds(h * PITCH, T), :].astype(bf16)
                part[seq * HEADS + h] = lax.dot_general(
                    key, value, (((0,), (0,)), ((), ())), preferred_element_type=f32
                )
                m = jnp.sum(key.astype(f32).reshape(T // 8, 8, D), axis=0)
                mass[pl.ds(seq * HEADS + h, 1), :] = jnp.sum(m, axis=0, keepdims=True)
            return carry

        lax.fori_loop(0, 8 // HG, group, 0)

    def core_copy(seq):
        return pltpu.make_async_remote_copy(
            src_ref=part.at[pl.ds(seq * HEADS + theirs, 8)], dst_ref=core_in.at[seq],
            send_sem=core_send.at[seq], recv_sem=core_recv.at[seq],
            device_id=(o, other), device_id_type=MESH,
        )

    def z_copy(seq, stage, half):
        peer = (first, second)[(stage + half) % 2]
        src, dst = ((zs1, zr1), (zs2, zr2))[stage]
        rows = pl.ds(4 * half, 4)
        return pltpu.make_async_remote_copy(
            src_ref=src.at[seq, rows], dst_ref=dst.at[seq, rows],
            send_sem=z_send.at[seq, stage, half], recv_sem=z_recv.at[seq, stage, half],
            device_id=(o, peer), device_id_type=MESH,
        )

    def state_copy(seq):
        rows = pl.ds(seq * HEADS + mine, 8)
        return pltpu.make_async_remote_copy(
            src_ref=state.at[rows], dst_ref=state.at[rows],
            send_sem=st_send.at[seq], recv_sem=st_recv.at[seq],
            device_id=(o, other), device_id_type=MESH,
        )

    def mass_copy(seq, d):
        return pltpu.make_async_remote_copy(
            src_ref=mass.at[pl.ds(seq * HEADS, HEADS)], dst_ref=mass_in.at[seq, d],
            send_sem=mass_send.at[seq, d], recv_sem=mass_recv.at[seq, d],
            device_id=(o, lax.rem(s + d, 8)), device_id_type=MESH,
        )

    def reduce(seq, stage):
        if stage == 0:
            core_copy(seq).wait_recv()
            extra, dst, at = core_in, zs1, 0
        elif stage == 1:
            extra, dst, at = zr1, zs2, 0
        else:
            extra, dst, at = zr2, state, seq * HEADS + mine
        if stage:
            z_copy(seq, stage - 1, 0).wait_recv()
            z_copy(seq, stage - 1, 1).wait_recv()

        def one(i, carry):
            for j in range(4):
                h = i * 4 + j
                total = part[seq * HEADS + mine + h] + extra[seq, h].astype(f32)
                if stage < 2:
                    part[seq * HEADS + mine + h] = total
                    dst[seq, h] = total.astype(bf16)
                else:
                    dst[at + h] = total.astype(bf16)
            return carry

        lax.fori_loop(0, 2, one, 0)
        if stage < 2:
            z_copy(seq, stage, 0).start()
            z_copy(seq, stage, 1).start()
        else:
            state_copy(seq).start()

    def local_state(seq):
        heads(seq, theirs)
        core_copy(seq).start()
        heads(seq, mine)
        for d in range(1, 8):
            mass_copy(seq, d).start()

    def take_mass(seq):
        for d in range(1, 8):
            mass_copy(seq, d).wait()
        rows = pl.ds(seq * HEADS, HEADS)
        total = mass[rows, :]
        for d in range(1, 8):
            total = total + mass_in[seq, d]
        mass[rows, :] = total

    def factors(seq):
        def group(i, carry):
            for j in range(HG):
                h = i * HG + j
                rows = pl.ds(h * PITCH, T)
                query = fa[rows, :].astype(bf16)
                q_head[seq * HEADS + h] = query
                m = mass[pl.ds(seq * HEADS + h, 1), :]
                bottom = jnp.sum(query.astype(f32) * m, axis=1, keepdims=True) + 0.001 * COUNT
                factor[seq, rows, :] = COUNT**0.5 / (bottom * factor[seq, rows, :])
            return carry

        lax.fori_loop(0, HEADS // HG, group, 0)

    def read(seq):
        state_copy(seq).wait_recv()

        def group(i, carry):
            for j in range(HG):
                h = i * HG + j
                top = jnp.dot(q_head[seq * HEADS + h], state[seq * HEADS + h], preferred_element_type=f32)
                columns = pl.ds(pl.multiple_of(h * D, D), D)
                mixed[seq, :, columns] = (top * factor[seq, pl.ds(h * PITCH, T), :]).astype(bf16)
            return carry

        lax.fori_loop(0, HEADS // HG, group, 0)
        pltpu.make_async_copy(mixed.at[seq], mixed_out.at[seq], out_sem.at[seq]).start()

    gate = lambda x: 1.0 + jnp.exp(-x)
    wait_load(0, 0)
    wait_load(1, 0)
    spread(k_nat, fa, 0, feature)
    spread(v_nat, fb, 0, lambda x: x)
    local_state(0)
    wait_load(0, 1)
    wait_load(1, 1)
    spread(k_nat, fa, 1, feature)
    spread(v_nat, fb, 1, lambda x: x)
    reduce(0, 0)
    local_state(1)
    service(0)
    wait_load(2, 0)
    wait_load(3, 0)
    spread(q_nat, fa, 0, feature)
    reduce(1, 0)
    spread(g_nat, factor.at[0], 0, gate)
    service(1)
    reduce(0, 1)
    take_mass(0)
    factors(0)
    reduce(1, 1)
    service(2)
    wait_load(2, 1)
    wait_load(3, 1)
    spread(q_nat, fa, 1, feature)
    spread(g_nat, factor.at[1], 1, gate)
    reduce(0, 2)
    take_mass(1)
    factors(1)
    reduce(1, 2)
    service(3)
    service(4)
    read(0)
    service(5)
    service(6)
    read(1)
    for i in range(7, len(groups)):
        service(i)
    for group in groups:
        for chunk in group:
            w_from_partner(*chunk)

    for item in sent:
        w_copy(*item).wait_send()
    for group in groups:
        for da, db, h in group:
            w_store(shard(da, db), core, h, da, db, 0).wait()
            w_store(shard(db, da), 1 - core, h, da, db, 1).wait()
    for c in range(2):
        for h in range(2):
            w_store(o, c, h, 0, 0, c).wait()
    for seq in range(SEQS):
        core_copy(seq).wait_send()
        state_copy(seq).wait_send()
        for stage in range(2):
            for half in range(2):
                z_copy(seq, stage, half).wait_send()
        pltpu.make_async_copy(mixed.at[seq], mixed_out.at[seq], out_sem.at[seq]).wait()


def body(queries_in, keys_in, values_in, gate_rows, out_weight):
    any_space = pl.BlockSpec(memory_space=pl.ANY)
    natural = pltpu.VMEM((SEQS, T, HEADS, D), bf16)
    wide = pltpu.VMEM((HEADS * PITCH, D), f32)
    exchange = pltpu.VMEM((SEQS, 8, D, D), bf16)
    dma = pltpu.SemaphoreType.DMA
    mixed, weight = pl.pallas_call(
        attention,
        out_shape=(
            jax.ShapeDtypeStruct((SEQS, T, WIDTH), bf16),
            jax.ShapeDtypeStruct((16, 2, 2, ROWS, WIDTH), bf16),
        ),
        in_specs=[any_space] * 5,
        out_specs=(any_space, any_space),
        scratch_shapes=[
            natural, natural, natural, natural,
            wide, wide, pltpu.VMEM((SEQS, HEADS * PITCH, D), f32),
            pltpu.VMEM((SEQS * HEADS, T, D), bf16),
            pltpu.VMEM((SEQS * HEADS, D, D), f32),
            pltpu.VMEM((SEQS * HEADS, D), f32),
            pltpu.VMEM((SEQS, 8, HEADS, D), f32),
            pltpu.VMEM((SEQS, 8, D, D), f32),
            exchange, exchange, exchange, exchange,
            pltpu.VMEM((SEQS * HEADS, D, D), bf16),
            pltpu.VMEM((SEQS, T, WIDTH), bf16),
            pltpu.VMEM((16, 2, 2, ROWS, WIDTH), bf16),
            dma((4, SEQS, PIECES)), dma, dma((SEQS,)),
            dma((SEQS,)), dma((SEQS,)), dma((SEQS, 2, 2)), dma((SEQS, 2, 2)),
            dma((SEQS,)), dma((SEQS,)), dma((SEQS, 8)), dma((SEQS, 8)),
            dma((5, 4, 4, 2)), dma((4, 4, 2)), dma((4, 4, 2)), dma((2, 4, 4, 2)),
        ],
        compiler_params=pltpu.CompilerParams(
            collective_id=0, has_side_effects=True, vmem_limit_bytes=63 * 1024 * 1024
        ),
        name="attention",
    )(queries_in, keys_in, values_in, gate_rows, out_weight.reshape(2, 2, ROWS, WIDTH))
    weight = weight.reshape(WIDTH, WIDTH)
    return jnp.einsum("btw,wv->btv", mixed, weight, preferred_element_type=f32).astype(bf16)


def solution(mesh):
    rows = P("outer", "span", None, None)
    return jax.shard_map(
        body, mesh=mesh, in_specs=(rows, rows, rows, rows, P("outer", None)),
        out_specs=P("outer", "span", None), check_vma=False,
    )
```

time: 124 us -> 62.4 us (0.50); the launches traced: 121 us -> 62.3 us
  Pallas kernels: 0 us -> 48.5 us
  blocking collectives: 25.3 us -> 0 us
  local copies, waits for them, and re-layouts: 22.5 us -> 0 us
  matrix products: 36.1 us -> 13.8 us
  waiting for transfers between devices: 18.6 us -> 0 us
  between operations: 14.9 us -> 0.01 us
  other arithmetic: 3.92 us -> 0 us
    pallas_call x0 -> x1, Pallas kernels: none -> 48.5 us  [body(): pl.pallas_call(attention, out_shape=(jax.ShapeDtypeStruct((SEQS, T, WIDTH...]
    psum x1 -> x0, blocking collectives: 25.3 us -> none  [body(): state, mass = lax.psum((part_state, part_mass), 'span')]
    unnamed x3 -> x0, local copies, waits for them, and re-layouts: 22.5 us -> none
    dot_general x4 -> x1, matrix products: 36.1 us -> 13.8 us  [body(): jnp.einsum('btw,wv->btv', mixed, weight, preferred_element_type=f32)]
    psum x1 -> x0, waiting for transfers between devices: 18.1 us -> none  [body(): state, mass = lax.psum((part_state, part_mass), 'span')]
    reduce_sum x1 -> x0, other arithmetic: 3.91 us -> none  [body(): part_mass = jnp.sum(key_feature.astype(jnp.float32), axis=1)]
  transfers between devices with their start and end apart: 2 -> 0, of which waited for: 1 -> 0; matrix products, arithmetic and copies ran while one was open for 27% -> 0% of each run, Pallas kernels for 0% -> 0%
where the time goes in v1:
time: 62.4 us; the launch traced here: 62.3 us
  Pallas kernels  48.5 us (78%)
  matrix products  13.8 us (22%)
    pallas_call x1, Pallas kernels, body(): pl.pallas_call(attention, out_shape=(jax.ShapeDtypeStruct((SEQS, T, WIDTH...  48.5 us
    dot_general x1, matrix products, body(): jnp.einsum('btw,wv->btv', mixed, weight, preferred_element_type=f32)  13.8 us

profile of v1, /device:TPU:1, one launch (start us, length us, event | category | flops | bytes accessed | tf_op | source)
XLA Modules:
  0.0 62.3 jit_solution(13639204575297673683)
XLA Ops:
  0.0 48.5 %attention.1 = (bf16[2,512,2048]{2,1,0:T(8,128)(2,1)}, bf16[16,2,2,32,2048]{4,3,2,1,0:T(8,128)(2,1)}) custom-call(bf16[2,512,16,128]{3,2,1,0:T(8,128)(2,1)} %q_in.1, bf16[2,512,16,128]{3,2,1,0:T(8,128)(2,1)} %k_in.1, bf16[2,512,16,128]{3,2,1,0:T(8,128)(2,1)} %v_in.1, bf16[2,512,16,128]{3,2,1,0:T(8,128)(2,1)} %g_in.1, bf16[2,2,32,2048]{3,2,1,0:T(8,128)(2,1)} %bitcast.6), custom_call_target="tpu_custom_call" | custom-call | tf_op jit(solution)/shard_map/attention/pallas_call | solution.py:376
  48.5 13.8 %convolution_convert_fusion = bf16[2,512,2048]{2,1,0:T(8,128)(2,1)} fusion(bf16[2,512,2048]{2,1,0:T(8,128)(2,1)} %get-tuple-element.7, bf16[2048,2048,1]{1,0,2:T(8,128)(2,1)} %bitcast.7), kind=kOutput, calls=%fused_computation | convolution fusion | flops 8592031744 | bytes 16777216 | tf_op jit(solution)/shard_map/btw,wv->btv/dot_general | solution.py:407

commit v2 on v0

v2 whole, which is shorter than its diff:
```python
import functools
import jax
import jax.numpy as jnp
from jax import lax
from jax.experimental import pallas as pl
from jax.experimental.pallas import tpu as pltpu
from jax.sharding import PartitionSpec as P

f32 = jnp.float32
bf16 = jnp.bfloat16
MESH = pl.DeviceIdType.MESH

SEQS = 2
T = 512
HEADS = 16
D = 128
WIDTH = HEADS * D
COUNT = 4096
PITCH = T + 4
TC = 64
HG = 4
PIECES = 4
ROWS = 32
CHUNKS = 4
CROWS = 4 * D

ORDER = (
    (3, 0, 0), (1, 0, 1), (0, 3, 0), (0, 1, 1), (3, 0, 1), (1, 0, 0), (0, 3, 1), (0, 1, 0),
    (2, 0, 0), (2, 0, 1), (3, 3, 0), (3, 1, 0), (1, 1, 1), (1, 3, 1), (0, 2, 0), (0, 2, 1),
    (3, 1, 1), (3, 3, 1), (1, 3, 0), (1, 1, 0), (2, 3, 0), (2, 1, 0), (2, 1, 1), (2, 3, 1),
    (3, 2, 0), (3, 2, 1), (1, 2, 0), (1, 2, 1), (2, 2, 0), (2, 2, 1),
)
ARRIVE = (
    4.7, 4.7, 4.7, 4.7, 7.5, 7.5, 7.5, 7.5, 10.3, 10.3, 10.3, 10.3, 11.7, 11.7, 13.1, 13.1,
    14.6, 14.6, 16.0, 16.0, 17.4, 17.4, 18.8, 18.8, 20.2, 21.6, 21.6, 21.6, 23.0, 23.0,
)
GROUPS = (
    ((0, 0), (3, 0), (1, 0), (0, 3), (0, 1), (2, 0), (0, 2), (3, 3)),
    ((3, 1), (1, 3), (1, 1), (2, 3), (3, 2), (2, 1), (1, 2), (2, 2)),
)


def make_plan():
    begin, weights_at = 2.0, 3.0
    units = []
    for seq in range(SEQS):
        for part in range(2):
            units.append((("key", seq, part), 0.5, ()))
        units.append((("value", seq), 0.35, ()))
        for group in range(2):
            for side in range(2):
                units.append((("heads", seq, group, side), 0.3, ()))
        units.append((("mass", seq), 0.05, ()))
    for seq in range(SEQS):
        for part in range(2):
            units.append((("query", seq, part), 0.5, ()))
        for part in range(2):
            units.append((("gate", seq, part), 0.4, ()))
        units.append((("take", seq), 0.15, ()))
        for part in range(4):
            units.append((("factor", seq, part), 0.35, ()))
    for seq in range(SEQS):
        for group in range(2):
            units.append((("last", 2 * seq + group), 0.02, (("sum", 4, 2 * seq + group),)))
        for part in range(4):
            units.append((("read", seq, part), 0.3, ()))
        for part in range(4):
            units.append((("project", 0, seq, part), 0.6, (("weight", 17),)))
    for seq in range(SEQS):
        for part in range(4):
            units.append((("project", 1, seq, part), 0.6, (("weight", 29),)))

    ready = {("weight", i): weights_at + at for i, at in enumerate(ARRIVE)}
    wire = (1.4, 0.7, 0.4, 0.7)
    plan, done, clock, at = [], set(), begin, 0
    while at < len(units) or ready:
        due = [e for e in ready if ready[e] <= clock]
        token = None
        if due:
            token = min(due, key=lambda e: (ready[e], e))
        elif at < len(units) and all(n in done for n in units[at][2]):
            token, cost, _ = units[at]
            at += 1
            clock += cost
            if token[0] == "heads" and token[3] == 0:
                ready["sum", 0, 2 * token[1] + token[2]] = clock + 1.6
        else:
            token = min(ready, key=lambda e: (ready[e], e))
            clock = ready[token]
        if token in ready:
            del ready[token]
            clock += 0.05 if token[0] == "weight" else (0.25, 0.15, 0.1, 0.02, 0.02)[token[1]]
            if token[0] == "sum" and token[1] < 4:
                ready["sum", token[1] + 1, token[2]] = clock + wire[token[1]] + 2.2
        done.add(token)
        plan.append(token)
    return plan


def feature(x):
    return jnp.maximum(x, 0.0) + jnp.exp(jnp.minimum(x, 0.0))


def spread(src, dst, seq, fn, low, high):
    def step(i, carry):
        start = i * TC
        values = fn(src[seq, pl.ds(start, TC)].astype(f32))
        for t in range(TC):
            for half in range(2):
                dst[pl.ds(start + t + 8 * half * PITCH, 8, stride=PITCH), :] = values[
                    t, 8 * half : 8 * half + 8, :
                ]
        return carry

    lax.fori_loop(low, high, step, 0)


def attention(
    q_in, k_in, v_in, g_in, w_in,
    out,
    q_nat, k_nat, v_nat, g_nat,
    fa, fb, factor, q_head, part, mass, mass_in,
    core_in, z1, z2, state, staged, w_buf,
    load_sem, w_load_sem, out_sem,
    core_send, core_recv, z_send, z_recv, st_send, st_recv, mass_send, mass_recv,
    ws_sem, wr_sem, wp_sem,
):
    o = lax.axis_index("outer")
    s = lax.axis_index("span")
    core = lax.rem(s, 2)
    z = lax.div(s, 2)
    other = s + 1 - 2 * core
    first = s + 2 * (1 - 2 * lax.rem(z, 2))
    second = 2 * (3 - z) + core
    upper = lax.div(z, 2)
    gray = lax.rem(z + upper, 2)
    sa = 1 + 3 * core
    sb = 4 - 3 * core
    a = lax.rem(lax.div(o, sa), 4)
    b = lax.rem(lax.div(o, sb), 4)

    def shard(da, db):
        return lax.rem(a + da, 4) * sa + lax.rem(b + db, 4) * sb

    arrays = (k_in, v_in, q_in, g_in)
    natural = (k_nat, v_nat, q_nat, g_nat)
    step = T // PIECES

    def load(i, seq, piece):
        rows = pl.ds(piece * step, step)
        return pltpu.make_async_copy(
            arrays[i].at[seq, rows], natural[i].at[seq, rows], load_sem.at[i, seq, piece]
        )

    own_w = pltpu.make_async_copy(w_in, w_buf.at[o], w_load_sem)
    own_w.start()
    for pair in ((0, 1), (2, 3)):
        for seq in range(SEQS):
            for i in pair:
                for piece in range(PIECES):
                    load(i, seq, piece).start()

    barrier = pltpu.get_barrier_semaphore()
    for da, db in ((1, 0), (3, 0), (0, 1), (0, 3)):
        pl.semaphore_signal(barrier, inc=1, device_id=(shard(da, db), s), device_id_type=MESH)
    for d in range(1, 8):
        pl.semaphore_signal(barrier, inc=1, device_id=(o, lax.rem(s + d, 8)), device_id_type=MESH)
    own_w.wait()
    pl.semaphore_wait(barrier, 11)

    kinds = {"A+": (1, 0), "A-": (3, 0), "B+": (0, 1), "B-": (0, 3)}
    sent = []

    def w_copy(kind, da, db, h):
        ref = w_buf.at[shard(da, db), core, h]
        if kind == "P":
            return pltpu.make_async_remote_copy(
                src_ref=ref, dst_ref=ref, send_sem=ws_sem.at[4, da, db, h], recv_sem=wp_sem.at[da, db, h],
                device_id=(o, other), device_id_type=MESH,
            )
        ka, kb = kinds[kind]
        return pltpu.make_async_remote_copy(
            src_ref=ref,
            dst_ref=ref,
            send_sem=ws_sem.at[list(kinds).index(kind), da, db, h],
            recv_sem=wr_sem.at[(da - ka) % 4, (db - kb) % 4, h],
            device_id=(shard(ka, kb), s),
            device_id_type=MESH,
        )

    def w_send(kind, da, db, h):
        w_copy(kind, da, db, h).start()
        sent.append((kind, da, db, h))

    def arrival(ref, sem):
        pltpu.make_async_remote_copy(
            src_ref=ref, dst_ref=ref, send_sem=ws_sem.at[0, 0, 0, 0], recv_sem=sem,
            device_id=(o, other), device_id_type=MESH,
        ).wait_recv()

    def w_arrive(da, db, h):
        arrival(w_buf.at[shard(da, db), core, h], wr_sem.at[da, db, h])
        if db == 0:
            if da == 3 and h == 0:
                w_send("A+", da, db, h)
            if da == 1 and h == 1:
                w_send("A-", da, db, h)
            w_send("B+", da, db, h)
            w_send("B-", da, db, h)
        elif db == 3 and h == 0:
            w_send("B+", da, db, h)
        elif db == 1 and h == 1:
            w_send("B-", da, db, h)
        w_send("P", da, db, h)

    for names, h in ((("A+", "B+"), 0), (("A-", "B-"), 1), (("A+", "B+"), 1), (("A-", "B-"), 0)):
        for name in names:
            w_send(name, 0, 0, h)

    mine = core * 8
    theirs = 8 - mine

    def heads(seq, base):
        for j in range(HG):
            h = base + j
            key = fa[pl.ds(h * PITCH, T), :].astype(bf16)
            value = fb[pl.ds(h * PITCH, T), :].astype(bf16)
            part[pl.ds((seq * HEADS + h) * D, D), :] = lax.dot_general(
                key, value, (((0,), (0,)), ((), ())), preferred_element_type=f32
            )
            m = jnp.sum(key.astype(f32).reshape(T // 8, 8, D), axis=0)
            mass[pl.ds(seq * HEADS + h, 1), :] = jnp.sum(m, axis=0, keepdims=True)

    def base_row(c, side):
        return ((c // 2) * HEADS + (theirs if side else mine) + 4 * (c % 2)) * D

    def core_copy(c):
        return pltpu.make_async_remote_copy(
            src_ref=part.at[pl.ds(base_row(c, 1), CROWS)], dst_ref=core_in.at[c],
            send_sem=core_send.at[c], recv_sem=core_recv.at[c],
            device_id=(o, other), device_id_type=MESH,
        )

    half_rows, quarter, eighth = CROWS // 2, CROWS // 4, CROWS // 8
    bits = ((gray, upper), (upper, gray))
    peers = ((first, second), (second, first))

    def kept(side, depth):
        at = side * half_rows
        if depth > 0:
            at = at + bits[side][0] * quarter
        if depth > 1:
            at = at + bits[side][1] * eighth
        return at

    def z_copy(c, stage, side):
        if stage == 0:
            src = part.at[pl.ds(base_row(c, 0) + side * half_rows + (1 - bits[side][0]) * quarter, quarter)]
            dst = z1.at[c, side]
        elif stage == 1:
            src = part.at[pl.ds(base_row(c, 0) + kept(side, 1) + (1 - bits[side][1]) * eighth, eighth)]
            dst = z2.at[c, side]
        else:
            rows = eighth if stage == 2 else quarter
            src = dst = state.at[pl.ds(base_row(c, 0) + kept(side, 2 if stage == 2 else 1), rows)]
        return pltpu.make_async_remote_copy(
            src_ref=src, dst_ref=dst, send_sem=z_send.at[c, stage, side], recv_sem=z_recv.at[c, stage, side],
            device_id=(o, peers[side][stage if stage < 2 else 3 - stage]), device_id_type=MESH,
        )

    def state_copy(c):
        rows = pl.ds(base_row(c, 0), CROWS)
        return pltpu.make_async_remote_copy(
            src_ref=state.at[rows], dst_ref=state.at[rows],
            send_sem=st_send.at[c], recv_sem=st_recv.at[c],
            device_id=(o, other), device_id_type=MESH,
        )

    def reduce(stage, c):
        if stage == 0:
            core_copy(c).wait_recv()
            rows = pl.ds(base_row(c, 0), CROWS)
            part[rows, :] = part[rows, :] + core_in[c]
        else:
            for side in range(2):
                z_copy(c, stage - 1, side).wait_recv()
                if stage < 3:
                    rows = pl.ds(base_row(c, 0) + kept(side, stage), quarter if stage == 1 else eighth)
                    total = part[rows, :] + (z1, z2)[stage - 1][c, side]
                    if stage == 1:
                        part[rows, :] = total
                    else:
                        state[rows, :] = total.astype(bf16)
        if stage < 4:
            for side in range(2):
                z_copy(c, stage, side).start()
        else:
            state_copy(c).start()

    def mass_copy(seq, d):
        return pltpu.make_async_remote_copy(
            src_ref=mass.at[pl.ds(seq * HEADS, HEADS)], dst_ref=mass_in.at[seq, d],
            send_sem=mass_send.at[seq, d], recv_sem=mass_recv.at[seq, d],
            device_id=(o, lax.rem(s + d, 8)), device_id_type=MESH,
        )

    def take_mass(seq):
        for d in range(1, 8):
            mass_copy(seq, d).wait()
        rows = pl.ds(seq * HEADS, HEADS)
        total = mass[rows, :]
        for d in range(1, 8):
            total = total + mass_in[seq, d]
        mass[rows, :] = total

    def factors(seq, group):
        for j in range(HG):
            h = group * HG + j
            rows = pl.ds(h * PITCH, T)
            query = fa[rows, :].astype(bf16)
            q_head[seq * HEADS + h] = query
            m = mass[pl.ds(seq * HEADS + h, 1), :]
            bottom = jnp.sum(query.astype(f32) * m, axis=1, keepdims=True) + 0.001 * COUNT
            factor[seq, rows, :] = COUNT**0.5 / (bottom * factor[seq, rows, :])

    def read(seq, group):
        for j in range(HG):
            h = seq * HEADS + group * HG + j
            top = jnp.dot(q_head[h], state[h * D : (h + 1) * D, :], preferred_element_type=f32)
            rows = pl.ds((group * HG + j) * PITCH, T)
            q_head[h] = (top * factor[seq, rows, :]).astype(bf16)

    def out_copy(seq, slab):
        columns = pl.ds(pl.multiple_of(slab * D, D), D)
        return pltpu.make_async_copy(
            staged.at[seq, slab], out.at[seq, :, columns], out_sem.at[seq, slab]
        )

    def project(half, seq, tiles):
        total = (fa, fb)[seq]
        names = [shard(da, db) for da, db in GROUPS[half]]
        left = jnp.concatenate([q_head[seq * HEADS + name] for name in names], axis=1)
        for tile in tiles:
            columns = slice(tile * 2 * D, (tile + 1) * 2 * D)
            right = jnp.concatenate(
                [w_buf[name, :, :, :, columns].reshape(D, 2 * D) for name in names], axis=0
            )
            result = jnp.dot(left, right, preferred_element_type=f32)
            for j in range(2):
                slab = 2 * tile + j
                piece = result[:, j * D : (j + 1) * D]
                rows = pl.ds(slab * PITCH, T)
                if half == 0:
                    total[rows, :] = piece
                else:
                    staged[seq, slab] = (total[rows, :] + piece).astype(bf16)
                    out_copy(seq, slab).start()

    loaded = set()

    def need(i, seq, pieces):
        for piece in pieces:
            if (i, seq, piece) not in loaded:
                loaded.add((i, seq, piece))
                load(i, seq, piece).wait()

    steps = T // TC // 2
    per = PIECES // 2
    gathered = set()
    for token in make_plan():
        kind, args = token[0], token[1:]
        if kind in ("key", "query", "gate"):
            seq, half = args
            source = {"key": 0, "query": 2, "gate": 3}[kind]
            need(source, seq, range(half * per, (half + 1) * per))
            spread(
                natural[source], factor.at[seq] if kind == "gate" else fa, seq,
                (lambda x: 1.0 + jnp.exp(-x)) if kind == "gate" else feature,
                half * steps, (half + 1) * steps,
            )
        elif kind == "value":
            need(1, args[0], range(PIECES))
            spread(v_nat, fb, args[0], lambda x: x, 0, T // TC)
        elif kind == "heads":
            seq, group, side = args
            heads(seq, (mine if side else theirs) + 4 * group)
            if side == 0:
                core_copy(2 * seq + group).start()
        elif kind == "mass":
            for d in range(1, 8):
                mass_copy(args[0], d).start()
        elif kind == "take":
            take_mass(*args)
        elif kind == "factor":
            factors(*args)
        elif kind == "sum":
            reduce(*args)
        elif kind == "weight":
            w_arrive(*ORDER[args[0]])
        elif kind == "last":
            state_copy(*args).wait_recv()
        elif kind == "read":
            read(*args)
        else:
            half, seq, quarter_of = args
            for da, db, h in ORDER:
                if (db, da) in GROUPS[half] and (da, db, h) not in gathered:
                    gathered.add((da, db, h))
                    arrival(w_buf.at[shard(db, da), 1 - core, h], wp_sem.at[da, db, h])
            project(half, seq, range(quarter_of * 2, quarter_of * 2 + 2))

    for item in sent:
        w_copy(*item).wait_send()
    for c in range(CHUNKS):
        core_copy(c).wait_send()
        state_copy(c).wait_send()
        for stage in range(4):
            for side in range(2):
                z_copy(c, stage, side).wait_send()
    for seq in range(SEQS):
        for slab in range(HEADS):
            out_copy(seq, slab).wait()


def body(queries_in, keys_in, values_in, gate_rows, out_weight):
    any_space = pl.BlockSpec(memory_space=pl.ANY)
    natural = pltpu.VMEM((SEQS, T, HEADS, D), bf16)
    wide = pltpu.VMEM((HEADS * PITCH, D), f32)
    dma = pltpu.SemaphoreType.DMA
    return pl.pallas_call(
        attention,
        out_shape=jax.ShapeDtypeStruct((SEQS, T, WIDTH), bf16),
        in_specs=[any_space] * 5,
        out_specs=any_space,
        scratch_shapes=[
            natural, natural, natural, natural,
            wide, wide, pltpu.VMEM((SEQS, HEADS * PITCH, D), f32),
            pltpu.VMEM((SEQS * HEADS, T, D), bf16),
            pltpu.VMEM((SEQS * HEADS * D, D), f32),
            pltpu.VMEM((SEQS * HEADS, D), f32),
            pltpu.VMEM((SEQS, 8, HEADS, D), f32),
            pltpu.VMEM((CHUNKS, CROWS, D), f32),
            pltpu.VMEM((CHUNKS, 2, CROWS // 4, D), f32),
            pltpu.VMEM((CHUNKS, 2, CROWS // 8, D), f32),
            pltpu.VMEM((SEQS * HEADS * D, D), bf16),
            pltpu.VMEM((SEQS, HEADS, T, D), bf16),
            pltpu.VMEM((16, 2, 2, ROWS, WIDTH), bf16),
            dma((4, SEQS, PIECES)), dma, dma((SEQS, HEADS)),
            dma((CHUNKS,)), dma((CHUNKS,)), dma((CHUNKS, 4, 2)), dma((CHUNKS, 4, 2)),
            dma((CHUNKS,)), dma((CHUNKS,)), dma((SEQS, 8)), dma((SEQS, 8)),
            dma((5, 4, 4, 2)), dma((4, 4, 2)), dma((4, 4, 2)),
        ],
        compiler_params=pltpu.CompilerParams(
            collective_id=0, has_side_effects=True, vmem_limit_bytes=63 * 1024 * 1024
        ),
        name="attention",
    )(queries_in, keys_in, values_in, gate_rows, out_weight.reshape(2, 2, ROWS, WIDTH))


def solution(mesh):
    rows = P("outer", "span", None, None)
    return jax.shard_map(
        body, mesh=mesh, in_specs=(rows, rows, rows, rows, P("outer", None)),
        out_specs=P("outer", "span", None), check_vma=False,
    )
```

time: 124 us -> 55.9 us (0.45); the launches traced: 121 us -> 55.7 us
  Pallas kernels: 0 us -> 50.9 us
  matrix products: 36.1 us -> 0 us
  blocking collectives: 25.3 us -> 0 us
  waiting for transfers between devices: 18.6 us -> 0 us
  local copies, waits for them, and re-layouts: 22.5 us -> 4.79 us
  between operations: 14.9 us -> 0.01 us
  other arithmetic: 3.92 us -> 0 us
    pallas_call x0 -> x1, Pallas kernels: none -> 50.9 us  [body(): pl.pallas_call(attention, out_shape=jax.ShapeDtypeStruct((SEQS, T, WIDTH)...]
    dot_general x4 -> x0, matrix products: 36.1 us -> none  [the longest x1 13.9 us: add_rows(): jnp.einsum('btw,wv->btv', part, piece, preferred_element_type=jnp.float32)]
    psum x1 -> x0, blocking collectives: 25.3 us -> none  [body(): state, mass = lax.psum((part_state, part_mass), 'span')]
    psum x1 -> x0, waiting for transfers between devices: 18.1 us -> none  [body(): state, mass = lax.psum((part_state, part_mass), 'span')]
    unnamed x3 -> x1, local copies, waits for them, and re-layouts: 22.5 us -> 4.79 us
    reduce_sum x1 -> x0, other arithmetic: 3.91 us -> none  [body(): part_mass = jnp.sum(key_feature.astype(jnp.float32), axis=1)]
  transfers between devices with their start and end apart: 2 -> 0, of which waited for: 1 -> 0; matrix products, arithmetic and copies ran while one was open for 27% -> 0% of each run, Pallas kernels for 0% -> 0%
where the time goes in v2:
time: 55.9 us; the launch traced here: 55.7 us
  Pallas kernels  50.9 us (91%)
  local copies, waits for them, and re-layouts  4.79 us (9%)
    pallas_call x1, Pallas kernels, body(): pl.pallas_call(attention, out_shape=jax.ShapeDtypeStruct((SEQS, T, WIDTH)...  50.9 us
    unnamed x1, local copies, waits for them, and re-layouts  4.79 us

profile of v2, /device:TPU:1, one launch (start us, length us, event | category | flops | bytes accessed | tf_op | source)
XLA Modules:
  0.0 55.7 jit_solution(16466093648573114677)
XLA Ops:
  0.0 50.9 %attention.1 = bf16[2,512,2048]{2,1,0:T(8,128)(2,1)} custom-call(bf16[2,512,16,128]{3,2,1,0:T(8,128)(2,1)} %q_in.1, bf16[2,512,16,128]{3,2,1,0:T(8,128)(2,1)} %k_in.1, bf16[2,512,16,128]{3,2,1,0:T(8,128)(2,1)} %v_in.1, bf16[2,512,16,128]{3,2,1,0:T(8,128)(2,1)} %g_in.1, bf16[2,2,32,2048]{3,2,1,0:T(8,128)(2,1)} %bitcast.1), custom_call_target="tpu_custom_call" | custom-call | tf_op jit(solution)/shard_map/attention/pallas_call | solution.py:430
  50.9 4.8 %copy.7 = bf16[2,512,2048]{2,1,0:T(8,128)(2,1)} copy(bf16[2,512,2048]{2,1,0:T(8,128)(2,1)} %attention.1) | data formatting | bytes 8388608

commit v3 on v2

--- a/solution.py
+++ b/solution.py
@@ -21,6 +21,7 @@
 HG = 4
 PIECES = 4
 ROWS = 32
+BLOCKS = 8
 CHUNKS = 4
 CROWS = 4 * D
 
@@ -31,8 +32,8 @@
     (3, 2, 0), (3, 2, 1), (1, 2, 0), (1, 2, 1), (2, 2, 0), (2, 2, 1),
 )
 ARRIVE = (
-    4.7, 4.7, 4.7, 4.7, 7.5, 7.5, 7.5, 7.5, 10.3, 10.3, 10.3, 10.3, 11.7, 11.7, 13.1, 13.1,
-    14.6, 14.6, 16.0, 16.0, 17.4, 17.4, 18.8, 18.8, 20.2, 21.6, 21.6, 21.6, 23.0, 23.0,
+    5.8, 5.8, 5.8, 5.8, 8.6, 8.6, 8.6, 8.6, 11.6, 11.6, 11.6, 11.6, 13.0, 13.0, 14.4, 14.4,
+    15.8, 15.8, 17.2, 17.2, 18.7, 18.7, 20.1, 20.1, 21.5, 22.9, 22.9, 22.9, 24.3, 24.5,
 )
 GROUPS = (
     ((0, 0), (3, 0), (1, 0), (0, 3), (0, 1), (2, 0), (0, 2), (3, 3)),
@@ -41,38 +42,38 @@
 
 
 def make_plan():
-    begin, weights_at = 2.0, 3.0
+    begin, weights_at, wire, hop = 2.5, 2.4, 1.4, 3.1
     units = []
     for seq in range(SEQS):
-        for part in range(2):
-            units.append((("key", seq, part), 0.5, ()))
+        for half in range(2):
+            units.append((("key", seq, half), 0.47, ()))
         units.append((("value", seq), 0.35, ()))
-        for group in range(2):
-            for side in range(2):
+        for side in range(2):
+            for group in range(2):
                 units.append((("heads", seq, group, side), 0.3, ()))
         units.append((("mass", seq), 0.05, ()))
     for seq in range(SEQS):
-        for part in range(2):
-            units.append((("query", seq, part), 0.5, ()))
-        for part in range(2):
-            units.append((("gate", seq, part), 0.4, ()))
+        for half in range(2):
+            units.append((("query", seq, half), 0.47, ()))
+        for half in range(2):
+            units.append((("gate", seq, half), 0.4, ()))
         units.append((("take", seq), 0.15, ()))
-        for part in range(4):
-            units.append((("factor", seq, part), 0.35, ()))
+        for group in range(4):
+            units.append((("factor", seq, group), 0.35, ()))
     for seq in range(SEQS):
         for group in range(2):
-            units.append((("last", 2 * seq + group), 0.02, (("sum", 4, 2 * seq + group),)))
-        for part in range(4):
-            units.append((("read", seq, part), 0.3, ()))
-        for part in range(4):
-            units.append((("project", 0, seq, part), 0.6, (("weight", 17),)))
+            c = 2 * seq + group
+            units.append((("last", c), 0.02, (("sum", 3, c),)))
+        for group in range(4):
+            units.append((("read", seq, group), 0.3, ()))
+        for quarter in range(4):
+            units.append((("project", 0, seq, quarter), 0.6, (("weight", 17),)))
     for seq in range(SEQS):
-        for part in range(4):
-            units.append((("project", 1, seq, part), 0.6, (("weight", 29),)))
+        for quarter in range(4):
+            units.append((("project", 1, seq, quarter), 0.6, (("weight", 29),)))
 
     ready = {("weight", i): weights_at + at for i, at in enumerate(ARRIVE)}
-    wire = (1.4, 0.7, 0.4, 0.7)
-    plan, done, clock, at = [], set(), begin, 0
+    plan, done, clock, at, link = [], set(), begin, 0, 0.0
     while at < len(units) or ready:
         due = [e for e in ready if ready[e] <= clock]
         token = None
@@ -89,11 +90,13 @@
             clock = ready[token]
         if token in ready:
             del ready[token]
-            clock += 0.05 if token[0] == "weight" else (0.25, 0.15, 0.1, 0.02, 0.02)[token[1]]
-            if token[0] == "sum" and token[1] < 4:
-                ready["sum", token[1] + 1, token[2]] = clock + wire[token[1]] + 2.2
+            clock += 0.05 if token[0] == "weight" else (0.25, 0.15, 0.15, 0.0)[token[1]]
+            if token[0] == "sum" and token[1] < 3:
+                link = max(link, clock) + wire
+                ready["sum", token[1] + 1, token[2]] = link + hop
         done.add(token)
-        plan.append(token)
+        if token[:2] != ("sum", 3):
+            plan.append(token)
     return plan
 
 
@@ -241,61 +244,56 @@
             device_id=(o, other), device_id_type=MESH,
         )
 
-    half_rows, quarter, eighth = CROWS // 2, CROWS // 4, CROWS // 8
-    bits = ((gray, upper), (upper, gray))
+    half_rows, quarter = CROWS // 2, CROWS // 4
+    bits = (gray, upper)
     peers = ((first, second), (second, first))
 
-    def kept(side, depth):
-        at = side * half_rows
-        if depth > 0:
-            at = at + bits[side][0] * quarter
-        if depth > 1:
-            at = at + bits[side][1] * eighth
-        return at
+    def quarter_row(side, keep):
+        bit = bits[side] if keep else 1 - bits[side]
+        return side * half_rows + bit * quarter
 
     def z_copy(c, stage, side):
-        if stage == 0:
-            src = part.at[pl.ds(base_row(c, 0) + side * half_rows + (1 - bits[side][0]) * quarter, quarter)]
-            dst = z1.at[c, side]
-        elif stage == 1:
-            src = part.at[pl.ds(base_row(c, 0) + kept(side, 1) + (1 - bits[side][1]) * eighth, eighth)]
-            dst = z2.at[c, side]
-        else:
-            rows = eighth if stage == 2 else quarter
-            src = dst = state.at[pl.ds(base_row(c, 0) + kept(side, 2 if stage == 2 else 1), rows)]
+        src = part.at[pl.ds(base_row(c, 0) + quarter_row(side, stage == 1), quarter)]
         return pltpu.make_async_remote_copy(
-            src_ref=src, dst_ref=dst, send_sem=z_send.at[c, stage, side], recv_sem=z_recv.at[c, stage, side],
-            device_id=(o, peers[side][stage if stage < 2 else 3 - stage]), device_id_type=MESH,
-        )
-
-    def state_copy(c):
-        rows = pl.ds(base_row(c, 0), CROWS)
+            src_ref=src, dst_ref=(z1, z2)[stage].at[c, side],
+            send_sem=z_send.at[c, stage, side], recv_sem=z_recv.at[c, stage, side],
+            device_id=(o, peers[side][stage]), device_id_type=MESH,
+        )
+
+    def state_copy(c, side, to):
+        rows = pl.ds(base_row(c, 0) + quarter_row(side, True), quarter)
+        peer = peers[side][0]
         return pltpu.make_async_remote_copy(
             src_ref=state.at[rows], dst_ref=state.at[rows],
-            send_sem=st_send.at[c], recv_sem=st_recv.at[c],
-            device_id=(o, other), device_id_type=MESH,
-        )
+            send_sem=st_send.at[c, side, to], recv_sem=st_recv.at[c, side, to],
+            device_id=(o, (peer, peer + 1 - 2 * core, other)[to]), device_id_type=MESH,
+        )
+
+    def take_state(c):
+        for side in range(2):
+            for to in range(3):
+                rows = pl.ds(base_row(c, int(to > 0)) + quarter_row(side, to == 2), quarter)
+                arrival(state.at[rows], st_recv.at[c, side, to])
 
     def reduce(stage, c):
         if stage == 0:
             core_copy(c).wait_recv()
             rows = pl.ds(base_row(c, 0), CROWS)
             part[rows, :] = part[rows, :] + core_in[c]
+            for side in range(2):
+                z_copy(c, 0, side).start()
         else:
             for side in range(2):
                 z_copy(c, stage - 1, side).wait_recv()
-                if stage < 3:
-                    rows = pl.ds(base_row(c, 0) + kept(side, stage), quarter if stage == 1 else eighth)
-                    total = part[rows, :] + (z1, z2)[stage - 1][c, side]
-                    if stage == 1:
-                        part[rows, :] = total
-                    else:
-                        state[rows, :] = total.astype(bf16)
-        if stage < 4:
-            for side in range(2):
-                z_copy(c, stage, side).start()
-        else:
-            state_copy(c).start()
+                rows = pl.ds(base_row(c, 0) + quarter_row(side, True), quarter)
+                total = part[rows, :] + (z1, z2)[stage - 1][c, side]
+                if stage == 1:
+                    part[rows, :] = total
+                    z_copy(c, 1, side).start()
+                else:
+                    state[rows, :] = total.astype(bf16)
+                    for to in range(3):
+                        state_copy(c, side, to).start()
 
     def mass_copy(seq, d):
         return pltpu.make_async_remote_copy(
@@ -398,7 +396,7 @@
         elif kind == "weight":
             w_arrive(*ORDER[args[0]])
         elif kind == "last":
-            state_copy(*args).wait_recv()
+            take_state(*args)
         elif kind == "read":
             read(*args)
         else:
@@ -413,13 +411,33 @@
         w_copy(*item).wait_send()
     for c in range(CHUNKS):
         core_copy(c).wait_send()
-        state_copy(c).wait_send()
-        for stage in range(4):
-            for side in range(2):
+        for side in range(2):
+            for stage in range(2):
                 z_copy(c, stage, side).wait_send()
+            for to in range(3):
+                state_copy(c, side, to).wait_send()
     for seq in range(SEQS):
         for slab in range(HEADS):
             out_copy(seq, slab).wait()
+
+
+def hand_over(src, dst, buffer, in_sem, out_sem):
+    blocks = [(seq, i) for seq in range(SEQS) for i in range(BLOCKS)]
+    rows = [pl.ds(i * (T // BLOCKS), T // BLOCKS) for i in range(BLOCKS)]
+
+    def fetch(seq, i):
+        return pltpu.make_async_copy(src.at[seq, rows[i]], buffer.at[seq, rows[i]], in_sem.at[seq, i])
+
+    def put(seq, i):
+        return pltpu.make_async_copy(buffer.at[seq, rows[i]], dst.at[seq, rows[i]], out_sem.at[seq, i])
+
+    for block in blocks:
+        fetch(*block).start()
+    for block in blocks:
+        fetch(*block).wait()
+        put(*block).start()
+    for block in blocks:
+        put(*block).wait()
 
 
 def body(queries_in, keys_in, values_in, gate_rows, out_weight):
@@ -427,7 +445,7 @@
     natural = pltpu.VMEM((SEQS, T, HEADS, D), bf16)
     wide = pltpu.VMEM((HEADS * PITCH, D), f32)
     dma = pltpu.SemaphoreType.DMA
-    return pl.pallas_call(
+    result = pl.pallas_call(
         attention,
         out_shape=jax.ShapeDtypeStruct((SEQS, T, WIDTH), bf16),
         in_specs=[any_space] * 5,
@@ -441,13 +459,13 @@
             pltpu.VMEM((SEQS, 8, HEADS, D), f32),
             pltpu.VMEM((CHUNKS, CROWS, D), f32),
             pltpu.VMEM((CHUNKS, 2, CROWS // 4, D), f32),
-            pltpu.VMEM((CHUNKS, 2, CROWS // 8, D), f32),
+            pltpu.VMEM((CHUNKS, 2, CROWS // 4, D), f32),
             pltpu.VMEM((SEQS * HEADS * D, D), bf16),
             pltpu.VMEM((SEQS, HEADS, T, D), bf16),
             pltpu.VMEM((16, 2, 2, ROWS, WIDTH), bf16),
             dma((4, SEQS, PIECES)), dma, dma((SEQS, HEADS)),
-            dma((CHUNKS,)), dma((CHUNKS,)), dma((CHUNKS, 4, 2)), dma((CHUNKS, 4, 2)),
-            dma((CHUNKS,)), dma((CHUNKS,)), dma((SEQS, 8)), dma((SEQS, 8)),
+            dma((CHUNKS,)), dma((CHUNKS,)), dma((CHUNKS, 2, 2)), dma((CHUNKS, 2, 2)),
+            dma((CHUNKS, 2, 3)), dma((CHUNKS, 2, 3)), dma((SEQS, 8)), dma((SEQS, 8)),
             dma((5, 4, 4, 2)), dma((4, 4, 2)), dma((4, 4, 2)),
         ],
         compiler_params=pltpu.CompilerParams(
@@ -455,6 +473,15 @@
         ),
         name="attention",
     )(queries_in, keys_in, values_in, gate_rows, out_weight.reshape(2, 2, ROWS, WIDTH))
+    return pl.pallas_call(
+        hand_over,
+        out_shape=jax.ShapeDtypeStruct((SEQS, T, WIDTH), bf16),
+        in_specs=[any_space],
+        out_specs=any_space,
+        scratch_shapes=[pltpu.VMEM((SEQS, T, WIDTH), bf16), dma((SEQS, BLOCKS)), dma((SEQS, BLOCKS))],
+        compiler_params=pltpu.CompilerParams(vmem_limit_bytes=63 * 1024 * 1024),
+        name="hand_over",
+    )(result)
 
 
 def solution(mesh):

time: 55.9 us -> 50.6 us (0.905)
  local copies, waits for them, and re-layouts: 4.79 us -> 0 us
  Pallas kernels: 50.9 us -> 50.3 us
    unnamed x1 -> x0, local copies, waits for them, and re-layouts: 4.79 us -> none
    pallas_call x1, Pallas kernels: 50.9 us -> 46.5 us  [body(): pl.pallas_call(attention, out_shape=jax.ShapeDtypeStruct((SEQS, T, WIDTH)...]
    pallas_call x0 -> x1, Pallas kernels: none -> 3.85 us  [body(): pl.pallas_call(hand_over, out_shape=jax.ShapeDtypeStruct((SEQS, T, WIDTH)...]
where the time goes in v3:
time: 50.6 us; the launch traced here: 50.5 us
  Pallas kernels  50.3 us (99%)
    pallas_call x1, Pallas kernels, body(): pl.pallas_call(attention, out_shape=jax.ShapeDtypeStruct((SEQS, T, WIDTH)...  46.5 us
    pallas_call x1, Pallas kernels, body(): pl.pallas_call(hand_over, out_shape=jax.ShapeDtypeStruct((SEQS, T, WIDTH)...  3.85 us

profile of v3, /device:TPU:1, one launch (start us, length us, event | category | flops | bytes accessed | tf_op | source)
XLA Modules:
  0.0 50.5 jit_solution(12184816005672793246)
XLA Ops:
  0.0 46.5 %attention.1.src = bf16[2,512,2048]{2,1,0:T(8,128)(2,1)} custom-call(bf16[2,512,16,128]{3,2,1,0:T(8,128)(2,1)} %q_in.1, bf16[2,512,16,128]{3,2,1,0:T(8,128)(2,1)} %k_in.1, bf16[2,512,16,128]{3,2,1,0:T(8,128)(2,1)} %v_in.1, bf16[2,512,16,128]{3,2,1,0:T(8,128)(2,1)} %g_in.1, bf16[2,2,32,2048]{3,2,1,0:T(8,128)(2,1)} %bitcast.1), custom_call_target="tpu_custom_call" | custom-call | tf_op jit(solution)/shard_map/attention/pallas_call | solution.py:448
  46.5 3.9 %hand_over.1 = bf16[2,512,2048]{2,1,0:T(8,128)(2,1)} custom-call(bf16[2,512,2048]{2,1,0:T(8,128)(2,1)} %attention.1.src), custom_call_target="tpu_custom_call" | custom-call | tf_op jit(solution)/shard_map/hand_over/pallas_call | solution.py:476

commit v4 on v3

--- a/solution.py
+++ b/solution.py
@@ -36,13 +36,13 @@
     15.8, 15.8, 17.2, 17.2, 18.7, 18.7, 20.1, 20.1, 21.5, 22.9, 22.9, 22.9, 24.3, 24.5,
 )
 GROUPS = (
-    ((0, 0), (3, 0), (1, 0), (0, 3), (0, 1), (2, 0), (0, 2), (3, 3)),
-    ((3, 1), (1, 3), (1, 1), (2, 3), (3, 2), (2, 1), (1, 2), (2, 2)),
+    ((0, 0), (3, 0), (1, 0), (0, 3), (0, 1), (2, 0), (0, 2), (3, 3), (3, 1), (1, 3)),
+    ((1, 1), (2, 3), (3, 2), (2, 1), (1, 2), (2, 2)),
 )
 
 
 def make_plan():
-    begin, weights_at, wire, hop = 2.5, 2.4, 1.4, 3.1
+    begin, weights_at, wire, hop = 2.5, 2.4, 1.4, 3.4
     units = []
     for seq in range(SEQS):
         for half in range(2):
@@ -60,28 +60,32 @@
         units.append((("take", seq), 0.15, ()))
         for group in range(4):
             units.append((("factor", seq, group), 0.35, ()))
+    first_work = len(units)
     for seq in range(SEQS):
         for group in range(2):
             c = 2 * seq + group
             units.append((("last", c), 0.02, (("sum", 3, c),)))
         for group in range(4):
-            units.append((("read", seq, group), 0.3, ()))
-        for quarter in range(4):
-            units.append((("project", 0, seq, quarter), 0.6, (("weight", 17),)))
-    for seq in range(SEQS):
-        for quarter in range(4):
-            units.append((("project", 1, seq, quarter), 0.6, (("weight", 29),)))
+            units.append((("read", seq, group), 0.3, (("last", 2 * seq), ("last", 2 * seq + 1))))
+    for half in range(2):
+        for seq in range(SEQS):
+            for quarter in range(4):
+                before = (("read", seq, 3),) if half == 0 else (("project", 0, seq, 3),)
+                units.append((("project", half, seq, quarter), (0.75, 0.48)[half], before + (("here", half),)))
 
     ready = {("weight", i): weights_at + at for i, at in enumerate(ARRIVE)}
-    plan, done, clock, at, link = [], set(), begin, 0, 0.0
-    while at < len(units) or ready:
+    plan, done, clock, link = [], set(), begin, 0.0
+    left = list(range(len(units)))
+    while left or ready:
         due = [e for e in ready if ready[e] <= clock]
-        token = None
+        able = [i for i in left if all(n in done for n in units[i][2])]
+        if left and left[0] < first_work:
+            able = left[:1]
         if due:
             token = min(due, key=lambda e: (ready[e], e))
-        elif at < len(units) and all(n in done for n in units[at][2]):
-            token, cost, _ = units[at]
-            at += 1
+        elif able:
+            left.remove(able[0])
+            token, cost, _ = units[able[0]]
             clock += cost
             if token[0] == "heads" and token[3] == 0:
                 ready["sum", 0, 2 * token[1] + token[2]] = clock + 1.6
@@ -90,12 +94,14 @@
             clock = ready[token]
         if token in ready:
             del ready[token]
-            clock += 0.05 if token[0] == "weight" else (0.25, 0.15, 0.15, 0.0)[token[1]]
+            clock += (0.25, 0.15, 0.15, 0.0)[token[1]] if token[0] == "sum" else 0.05
+            if token in (("weight", 18), ("weight", 29)):
+                ready["here", int(token[1] == 29)] = clock + 1.6
             if token[0] == "sum" and token[1] < 3:
                 link = max(link, clock) + wire
                 ready["sum", token[1] + 1, token[2]] = link + hop
         done.add(token)
-        if token[:2] != ("sum", 3):
+        if token[:2] != ("sum", 3) and token[0] != "here":
             plan.append(token)
     return plan
 

time: 50.6 us -> 50.8 us (level)
  no operation moved by 1% of the time
where the time goes in v4:
time: 50.8 us; the launch traced here: 50.7 us
  Pallas kernels  50.6 us (100%)
    pallas_call x1, Pallas kernels, body(): pl.pallas_call(attention, out_shape=jax.ShapeDtypeStruct((SEQS, T, WIDTH)...  46.7 us
    pallas_call x1, Pallas kernels, body(): pl.pallas_call(hand_over, out_shape=jax.ShapeDtypeStruct((SEQS, T, WIDTH)...  3.85 us

profile of v4, /device:TPU:1, one launch (start us, length us, event | category | flops | bytes accessed | tf_op | source)
XLA Modules:
  0.0 50.7 jit_solution(6152508830684563877)
XLA Ops:
  0.0 46.7 %attention.1.src = bf16[2,512,2048]{2,1,0:T(8,128)(2,1)} custom-call(bf16[2,512,16,128]{3,2,1,0:T(8,128)(2,1)} %q_in.1, bf16[2,512,16,128]{3,2,1,0:T(8,128)(2,1)} %k_in.1, bf16[2,512,16,128]{3,2,1,0:T(8,128)(2,1)} %v_in.1, bf16[2,512,16,128]{3,2,1,0:T(8,128)(2,1)} %g_in.1, bf16[2,2,32,2048]{3,2,1,0:T(8,128)(2,1)} %bitcast.1), custom_call_target="tpu_custom_call" | custom-call | tf_op jit(solution)/shard_map/attention/pallas_call | solution.py:454
  46.7 3.9 %hand_over.1 = bf16[2,512,2048]{2,1,0:T(8,128)(2,1)} custom-call(bf16[2,512,2048]{2,1,0:T(8,128)(2,1)} %attention.1.src), custom_call_target="tpu_custom_call" | custom-call | tf_op jit(solution)/shard_map/hand_over/pallas_call | solution.py:482

commit v5 on v4

--- a/solution.py
+++ b/solution.py
@@ -21,7 +21,6 @@
 HG = 4
 PIECES = 4
 ROWS = 32
-BLOCKS = 8
 CHUNKS = 4
 CROWS = 4 * D
 
@@ -40,6 +39,8 @@
     ((1, 1), (2, 3), (3, 2), (2, 1), (1, 2), (2, 2)),
 )
 
+LATE = len(GROUPS[1])
+
 
 def make_plan():
     begin, weights_at, wire, hop = 2.5, 2.4, 1.4, 3.4
@@ -67,11 +68,9 @@
             units.append((("last", c), 0.02, (("sum", 3, c),)))
         for group in range(4):
             units.append((("read", seq, group), 0.3, (("last", 2 * seq), ("last", 2 * seq + 1))))
-    for half in range(2):
-        for seq in range(SEQS):
-            for quarter in range(4):
-                before = (("read", seq, 3),) if half == 0 else (("project", 0, seq, 3),)
-                units.append((("project", half, seq, quarter), (0.75, 0.48)[half], before + (("here", half),)))
+    for seq in range(SEQS):
+        for quarter in range(4):
+            units.append((("project", seq, quarter), 0.75, (("read", seq, 3), ("here", 0))))
 
     ready = {("weight", i): weights_at + at for i, at in enumerate(ARRIVE)}
     plan, done, clock, link = [], set(), begin, 0.0
@@ -95,8 +94,8 @@
         if token in ready:
             del ready[token]
             clock += (0.25, 0.15, 0.15, 0.0)[token[1]] if token[0] == "sum" else 0.05
-            if token in (("weight", 18), ("weight", 29)):
-                ready["here", int(token[1] == 29)] = clock + 1.6
+            if token == ("weight", 18):
+                ready["here", 0] = clock + 1.6
             if token[0] == "sum" and token[1] < 3:
                 link = max(link, clock) + wire
                 ready["sum", token[1] + 1, token[2]] = link + hop
@@ -126,11 +125,11 @@
 
 def attention(
     q_in, k_in, v_in, g_in, w_in,
-    out,
+    sum_out, mixed_out, w_out,
     q_nat, k_nat, v_nat, g_nat,
     fa, fb, factor, q_head, part, mass, mass_in,
-    core_in, z1, z2, state, staged, w_buf,
-    load_sem, w_load_sem, out_sem,
+    core_in, z1, z2, state, w_buf,
+    load_sem, w_load_sem, sum_sem, mixed_sem, w_out_sem,
     core_send, core_recv, z_send, z_recv, st_send, st_recv, mass_send, mass_recv,
     ws_sem, wr_sem, wp_sem,
 ):
@@ -221,6 +220,13 @@
         elif db == 1 and h == 1:
             w_send("B-", da, db, h)
         w_send("P", da, db, h)
+        if (da, db) in GROUPS[1]:
+            w_store(GROUPS[1].index((da, db)), core, h, 0).start()
+
+    def w_store(i, c, h, which):
+        return pltpu.make_async_copy(
+            w_buf.at[shard(*GROUPS[1][i]), c, h], w_out.at[i, c, h], w_out_sem.at[i, h, which]
+        )
 
     for names, h in ((("A+", "B+"), 0), (("A-", "B-"), 1), (("A+", "B+"), 1), (("A-", "B-"), 0)):
         for name in names:
@@ -334,15 +340,19 @@
             rows = pl.ds((group * HG + j) * PITCH, T)
             q_head[h] = (top * factor[seq, rows, :]).astype(bf16)
 
-    def out_copy(seq, slab):
-        columns = pl.ds(pl.multiple_of(slab * D, D), D)
+    def mixed_copy(seq, i):
         return pltpu.make_async_copy(
-            staged.at[seq, slab], out.at[seq, :, columns], out_sem.at[seq, slab]
-        )
-
-    def project(half, seq, tiles):
+            q_head.at[seq * HEADS + shard(*GROUPS[1][i])], mixed_out.at[seq, i], mixed_sem.at[seq, i]
+        )
+
+    def sum_copy(seq, slab):
+        return pltpu.make_async_copy(
+            (fa, fb)[seq].at[pl.ds(slab * PITCH, T)], sum_out.at[seq, slab], sum_sem.at[seq, slab]
+        )
+
+    def project(seq, tiles):
         total = (fa, fb)[seq]
-        names = [shard(da, db) for da, db in GROUPS[half]]
+        names = [shard(da, db) for da, db in GROUPS[0]]
         left = jnp.concatenate([q_head[seq * HEADS + name] for name in names], axis=1)
         for tile in tiles:
             columns = slice(tile * 2 * D, (tile + 1) * 2 * D)
@@ -352,13 +362,8 @@
             result = jnp.dot(left, right, preferred_element_type=f32)
             for j in range(2):
                 slab = 2 * tile + j
-                piece = result[:, j * D : (j + 1) * D]
-                rows = pl.ds(slab * PITCH, T)
-                if half == 0:
-                    total[rows, :] = piece
-                else:
-                    staged[seq, slab] = (total[rows, :] + piece).astype(bf16)
-                    out_copy(seq, slab).start()
+                total[pl.ds(slab * PITCH, T), :] = result[:, j * D : (j + 1) * D]
+                sum_copy(seq, slab).start()
 
     loaded = set()
 
@@ -371,6 +376,16 @@
     steps = T // TC // 2
     per = PIECES // 2
     gathered = set()
+
+    def from_other_core(group):
+        for da, db, h in ORDER:
+            place = (db, da)
+            if place in GROUPS[group] and (da, db, h) not in gathered:
+                gathered.add((da, db, h))
+                arrival(w_buf.at[shard(*place), 1 - core, h], wp_sem.at[da, db, h])
+                if group == 1:
+                    w_store(GROUPS[1].index(place), 1 - core, h, 1).start()
+
     for token in make_plan():
         kind, args = token[0], token[1:]
         if kind in ("key", "query", "gate"):
@@ -405,13 +420,14 @@
             take_state(*args)
         elif kind == "read":
             read(*args)
+            if args[1] == HEADS // HG - 1:
+                for i in range(LATE):
+                    mixed_copy(args[0], i).start()
         else:
-            half, seq, quarter_of = args
-            for da, db, h in ORDER:
-                if (db, da) in GROUPS[half] and (da, db, h) not in gathered:
-                    gathered.add((da, db, h))
-                    arrival(w_buf.at[shard(db, da), 1 - core, h], wp_sem.at[da, db, h])
-            project(half, seq, range(quarter_of * 2, quarter_of * 2 + 2))
+            seq, quarter_of = args
+            from_other_core(0)
+            project(seq, range(quarter_of * 2, quarter_of * 2 + 2))
+    from_other_core(1)
 
     for item in sent:
         w_copy(*item).wait_send()
@@ -424,26 +440,52 @@
                 state_copy(c, side, to).wait_send()
     for seq in range(SEQS):
         for slab in range(HEADS):
-            out_copy(seq, slab).wait()
-
-
-def hand_over(src, dst, buffer, in_sem, out_sem):
-    blocks = [(seq, i) for seq in range(SEQS) for i in range(BLOCKS)]
-    rows = [pl.ds(i * (T // BLOCKS), T // BLOCKS) for i in range(BLOCKS)]
-
-    def fetch(seq, i):
-        return pltpu.make_async_copy(src.at[seq, rows[i]], buffer.at[seq, rows[i]], in_sem.at[seq, i])
-
-    def put(seq, i):
-        return pltpu.make_async_copy(buffer.at[seq, rows[i]], dst.at[seq, rows[i]], out_sem.at[seq, i])
-
-    for block in blocks:
-        fetch(*block).start()
-    for block in blocks:
-        fetch(*block).wait()
-        put(*block).start()
-    for block in blocks:
-        put(*block).wait()
+            sum_copy(seq, slab).wait()
+        for i in range(LATE):
+            mixed_copy(seq, i).wait()
+    for i in range(LATE):
+        for h in range(2):
+            w_store(i, core, h, 0).wait()
+            w_store(i, 1 - core, h, 1).wait()
+
+
+def finish(sums, mixed, weight, out, sum_buf, mixed_buf, w_buf, staged, sum_sem, mixed_sem, w_sem, out_sem):
+    def take_w(i):
+        return pltpu.make_async_copy(weight.at[i], w_buf.at[i], w_sem.at[i])
+
+    def take_mixed(seq):
+        return pltpu.make_async_copy(mixed.at[seq], mixed_buf.at[seq], mixed_sem.at[seq])
+
+    def take_sum(seq, slab):
+        return pltpu.make_async_copy(sums.at[seq, slab], sum_buf.at[seq, slab], sum_sem.at[seq, slab])
+
+    def put(seq, slab):
+        columns = pl.ds(slab * D, D)
+        return pltpu.make_async_copy(staged.at[seq, slab], out.at[seq, :, columns], out_sem.at[seq, slab])
+
+    for i in range(LATE):
+        take_w(i).start()
+    for seq in range(SEQS):
+        take_mixed(seq).start()
+        for slab in range(HEADS):
+            take_sum(seq, slab).start()
+    for i in range(LATE):
+        take_w(i).wait()
+    for seq in range(SEQS):
+        take_mixed(seq).wait()
+        left = jnp.concatenate([mixed_buf[seq, i] for i in range(LATE)], axis=1)
+        for tile in range(HEADS // 2):
+            columns = slice(tile * 2 * D, (tile + 1) * 2 * D)
+            right = w_buf[:, :, :, :, columns].reshape(LATE * D, 2 * D)
+            result = jnp.dot(left, right, preferred_element_type=f32)
+            for j in range(2):
+                slab = 2 * tile + j
+                take_sum(seq, slab).wait()
+                staged[seq, slab] = (sum_buf[seq, slab] + result[:, j * D : (j + 1) * D]).astype(bf16)
+                put(seq, slab).start()
+    for seq in range(SEQS):
+        for slab in range(HEADS):
+            put(seq, slab).wait()
 
 
 def body(queries_in, keys_in, values_in, gate_rows, out_weight):
@@ -451,11 +493,16 @@
     natural = pltpu.VMEM((SEQS, T, HEADS, D), bf16)
     wide = pltpu.VMEM((HEADS * PITCH, D), f32)
     dma = pltpu.SemaphoreType.DMA
-    result = pl.pallas_call(
+    shapes = (
+        ((SEQS, HEADS, T, D), f32),
+        ((SEQS, LATE, T, D), bf16),
+        ((LATE, 2, 2, ROWS, WIDTH), bf16),
+    )
+    late = pl.pallas_call(
         attention,
-        out_shape=jax.ShapeDtypeStruct((SEQS, T, WIDTH), bf16),
+        out_shape=tuple(jax.ShapeDtypeStruct(*shape) for shape in shapes),
         in_specs=[any_space] * 5,
-        out_specs=any_space,
+        out_specs=(any_space,) * 3,
         scratch_shapes=[
             natural, natural, natural, natural,
             wide, wide, pltpu.VMEM((SEQS, HEADS * PITCH, D), f32),
@@ -467,9 +514,8 @@
             pltpu.VMEM((CHUNKS, 2, CROWS // 4, D), f32),
             pltpu.VMEM((CHUNKS, 2, CROWS // 4, D), f32),
             pltpu.VMEM((SEQS * HEADS * D, D), bf16),
-            pltpu.VMEM((SEQS, HEADS, T, D), bf16),
             pltpu.VMEM((16, 2, 2, ROWS, WIDTH), bf16),
-            dma((4, SEQS, PIECES)), dma, dma((SEQS, HEADS)),
+            dma((4, SEQS, PIECES)), dma, dma((SEQS, HEADS)), dma((SEQS, LATE)), dma((LATE, 2, 2)),
             dma((CHUNKS,)), dma((CHUNKS,)), dma((CHUNKS, 2, 2)), dma((CHUNKS, 2, 2)),
             dma((CHUNKS, 2, 3)), dma((CHUNKS, 2, 3)), dma((SEQS, 8)), dma((SEQS, 8)),
             dma((5, 4, 4, 2)), dma((4, 4, 2)), dma((4, 4, 2)),
@@ -480,14 +526,17 @@
         name="attention",
     )(queries_in, keys_in, values_in, gate_rows, out_weight.reshape(2, 2, ROWS, WIDTH))
     return pl.pallas_call(
-        hand_over,
+        finish,
         out_shape=jax.ShapeDtypeStruct((SEQS, T, WIDTH), bf16),
-        in_specs=[any_space],
+        in_specs=[any_space] * 3,
         out_specs=any_space,
-        scratch_shapes=[pltpu.VMEM((SEQS, T, WIDTH), bf16), dma((SEQS, BLOCKS)), dma((SEQS, BLOCKS))],
+        scratch_shapes=[pltpu.VMEM(*shape) for shape in shapes] + [
+            pltpu.VMEM((SEQS, HEADS, T, D), bf16),
+            dma((SEQS, HEADS)), dma((SEQS,)), dma((LATE,)), dma((SEQS, HEADS)),
+        ],
         compiler_params=pltpu.CompilerParams(vmem_limit_bytes=63 * 1024 * 1024),
-        name="hand_over",
-    )(result)
+        name="finish",
+    )(*late)
 
 
 def solution(mesh):

time: 50.8 us -> 59.8 us (1.18)
  Pallas kernels: 50.6 us -> 59.5 us
    pallas_call x2, Pallas kernels: 50.6 us -> 59.5 us  [the longest x1 44.5 us: body(): pl.pallas_call(attention, out_shape=tuple((jax.ShapeDtypeStruct(*shape) f...]
where the time goes in v5:
time: 59.8 us; the launch traced here: 59.7 us
  Pallas kernels  59.5 us (99%)
    pallas_call x1, Pallas kernels, body(): pl.pallas_call(attention, out_shape=tuple((jax.ShapeDtypeStruct(*shape) f...  44.5 us
    pallas_call x1, Pallas kernels, body(): pl.pallas_call(finish, out_shape=jax.ShapeDtypeStruct((SEQS, T, WIDTH), b...  15 us

profile of v5, /device:TPU:1, one launch (start us, length us, event | category | flops | bytes accessed | tf_op | source)
XLA Modules:
  0.0 59.7 jit_solution(5836151799823437237)
XLA Ops:
  0.0 44.5 %attention.1 = (f32[2,16,512,128]{3,2,1,0:T(8,128)}, bf16[2,6,512,128]{3,2,1,0:T(8,128)(2,1)}, bf16[6,2,2,32,2048]{4,3,2,1,0:T(8,128)(2,1)}) custom-call(bf16[2,512,16,128]{3,2,1,0:T(8,128)(2,1)} %q_in.1, bf16[2,512,16,128]{3,2,1,0:T(8,128)(2,1)} %k_in.1, bf16[2,512,16,128]{3,2,1,0:T(8,128)(2,1)} %v_in.1, bf16[2,512,16,128]{3,2,1,0:T(8,128)(2,1)} %g_in.1, ...), custom_call_target="tpu_custom_call" | custom-call | tf_op jit(solution)/shard_map/attention/pallas_call | solution.py:501
  44.5 15.0 %finish.1 = bf16[2,512,2048]{2,1,0:T(8,128)(2,1)} custom-call(f32[2,16,512,128]{3,2,1,0:T(8,128)} %get-tuple-element.8.sums, bf16[2,6,512,128]{3,2,1,0:T(8,128)(2,1)} %get-tuple-element.9.mixed, bf16[6,2,2,32,2048]{4,3,2,1,0:T(8,128)(2,1)} %get-tuple-element.10.weight), custom_call_target="tpu_custom_call" | custom-call | tf_op jit(solution)/shard_map/finish/pallas_call | solution.py:528

commit v6 on v5

--- a/solution.py
+++ b/solution.py
@@ -17,8 +17,8 @@
 WIDTH = HEADS * D
 COUNT = 4096
 PITCH = T + 4
-TC = 64
-HG = 4
+TC = 32
+HG = 2
 PIECES = 4
 ROWS = 32
 CHUNKS = 4
@@ -59,18 +59,18 @@
         for half in range(2):
             units.append((("gate", seq, half), 0.4, ()))
         units.append((("take", seq), 0.15, ()))
-        for group in range(4):
-            units.append((("factor", seq, group), 0.35, ()))
+        for group in range(2):
+            units.append((("factor", seq, group), 0.7, ()))
     first_work = len(units)
     for seq in range(SEQS):
         for group in range(2):
             c = 2 * seq + group
             units.append((("last", c), 0.02, (("sum", 3, c),)))
-        for group in range(4):
-            units.append((("read", seq, group), 0.3, (("last", 2 * seq), ("last", 2 * seq + 1))))
+        for group in range(2):
+            units.append((("read", seq, group), 0.6, (("last", 2 * seq), ("last", 2 * seq + 1))))
     for seq in range(SEQS):
-        for quarter in range(4):
-            units.append((("project", seq, quarter), 0.75, (("read", seq, 3), ("here", 0))))
+        for half in range(2):
+            units.append((("project", seq, half), 1.5, (("read", seq, 1), ("here", 0))))
 
     ready = {("weight", i): weights_at + at for i, at in enumerate(ARRIVE)}
     plan, done, clock, link = [], set(), begin, 0.0
@@ -235,9 +235,17 @@
     mine = core * 8
     theirs = 8 - mine
 
+    def in_steps(count, one):
+        def body(i, carry):
+            for j in range(HG):
+                one(i * HG + j)
+            return carry
+
+        lax.fori_loop(0, count // HG, body, 0)
+
     def heads(seq, base):
-        for j in range(HG):
-            h = base + j
+        def one(i):
+            h = base + i
             key = fa[pl.ds(h * PITCH, T), :].astype(bf16)
             value = fb[pl.ds(h * PITCH, T), :].astype(bf16)
             part[pl.ds((seq * HEADS + h) * D, D), :] = lax.dot_general(
@@ -245,6 +253,8 @@
             )
             m = jnp.sum(key.astype(f32).reshape(T // 8, 8, D), axis=0)
             mass[pl.ds(seq * HEADS + h, 1), :] = jnp.sum(m, axis=0, keepdims=True)
+
+        in_steps(4, one)
 
     def base_row(c, side):
         return ((c // 2) * HEADS + (theirs if side else mine) + 4 * (c % 2)) * D
@@ -324,8 +334,8 @@
         mass[rows, :] = total
 
     def factors(seq, group):
-        for j in range(HG):
-            h = group * HG + j
+        def one(i):
+            h = group * 8 + i
             rows = pl.ds(h * PITCH, T)
             query = fa[rows, :].astype(bf16)
             q_head[seq * HEADS + h] = query
@@ -333,12 +343,17 @@
             bottom = jnp.sum(query.astype(f32) * m, axis=1, keepdims=True) + 0.001 * COUNT
             factor[seq, rows, :] = COUNT**0.5 / (bottom * factor[seq, rows, :])
 
+        in_steps(8, one)
+
     def read(seq, group):
-        for j in range(HG):
-            h = seq * HEADS + group * HG + j
-            top = jnp.dot(q_head[h], state[h * D : (h + 1) * D, :], preferred_element_type=f32)
-            rows = pl.ds((group * HG + j) * PITCH, T)
+        def one(i):
+            h = seq * HEADS + group * 8 + i
+            block = state[pl.ds(pl.multiple_of(h * D, D), D), :]
+            top = jnp.dot(q_head[h], block, preferred_element_type=f32)
+            rows = pl.ds((group * 8 + i) * PITCH, T)
             q_head[h] = (top * factor[seq, rows, :]).astype(bf16)
+
+        in_steps(8, one)
 
     def mixed_copy(seq, i):
         return pltpu.make_async_copy(
@@ -350,12 +365,13 @@
             (fa, fb)[seq].at[pl.ds(slab * PITCH, T)], sum_out.at[seq, slab], sum_sem.at[seq, slab]
         )
 
-    def project(seq, tiles):
+    def project(seq, low, high):
         total = (fa, fb)[seq]
         names = [shard(da, db) for da, db in GROUPS[0]]
-        left = jnp.concatenate([q_head[seq * HEADS + name] for name in names], axis=1)
-        for tile in tiles:
-            columns = slice(tile * 2 * D, (tile + 1) * 2 * D)
+
+        def tile_of(tile, carry):
+            left = jnp.concatenate([q_head[seq * HEADS + name] for name in names], axis=1)
+            columns = pl.ds(pl.multiple_of(tile * 2 * D, 2 * D), 2 * D)
             right = jnp.concatenate(
                 [w_buf[name, :, :, :, columns].reshape(D, 2 * D) for name in names], axis=0
             )
@@ -364,6 +380,9 @@
                 slab = 2 * tile + j
                 total[pl.ds(slab * PITCH, T), :] = result[:, j * D : (j + 1) * D]
                 sum_copy(seq, slab).start()
+            return carry
+
+        lax.fori_loop(low, high, tile_of, 0)
 
     loaded = set()
 
@@ -420,13 +439,13 @@
             take_state(*args)
         elif kind == "read":
             read(*args)
-            if args[1] == HEADS // HG - 1:
+            if args[1] == 1:
                 for i in range(LATE):
                     mixed_copy(args[0], i).start()
         else:
-            seq, quarter_of = args
+            seq, half = args
             from_other_core(0)
-            project(seq, range(quarter_of * 2, quarter_of * 2 + 2))
+            project(seq, 4 * half, 4 * half + 4)
     from_other_core(1)
 
     for item in sent:
@@ -460,32 +479,46 @@
         return pltpu.make_async_copy(sums.at[seq, slab], sum_buf.at[seq, slab], sum_sem.at[seq, slab])
 
     def put(seq, slab):
-        columns = pl.ds(slab * D, D)
+        columns = pl.ds(pl.multiple_of(slab * D, D), D)
         return pltpu.make_async_copy(staged.at[seq, slab], out.at[seq, :, columns], out_sem.at[seq, slab])
 
     for i in range(LATE):
         take_w(i).start()
-    for seq in range(SEQS):
+
+    def start(seq, carry):
         take_mixed(seq).start()
-        for slab in range(HEADS):
-            take_sum(seq, slab).start()
+        lax.fori_loop(0, HEADS, lambda slab, c: (take_sum(seq, slab).start(), c)[1], 0)
+        return carry
+
+    lax.fori_loop(0, SEQS, start, 0)
     for i in range(LATE):
         take_w(i).wait()
-    for seq in range(SEQS):
-        take_mixed(seq).wait()
+
+    def one(step, carry):
+        seq, tile = lax.div(step, HEADS // 2), lax.rem(step, HEADS // 2)
+
+        @pl.when(tile == 0)
+        def _():
+            take_mixed(seq).wait()
+
         left = jnp.concatenate([mixed_buf[seq, i] for i in range(LATE)], axis=1)
-        for tile in range(HEADS // 2):
-            columns = slice(tile * 2 * D, (tile + 1) * 2 * D)
-            right = w_buf[:, :, :, :, columns].reshape(LATE * D, 2 * D)
-            result = jnp.dot(left, right, preferred_element_type=f32)
-            for j in range(2):
-                slab = 2 * tile + j
-                take_sum(seq, slab).wait()
-                staged[seq, slab] = (sum_buf[seq, slab] + result[:, j * D : (j + 1) * D]).astype(bf16)
-                put(seq, slab).start()
-    for seq in range(SEQS):
-        for slab in range(HEADS):
-            put(seq, slab).wait()
+        columns = pl.ds(pl.multiple_of(tile * 2 * D, 2 * D), 2 * D)
+        right = w_buf[:, :, :, :, columns].reshape(LATE * D, 2 * D)
+        result = jnp.dot(left, right, preferred_element_type=f32)
+        for j in range(2):
+            slab = 2 * tile + j
+            take_sum(seq, slab).wait()
+            staged[seq, slab] = (sum_buf[seq, slab] + result[:, j * D : (j + 1) * D]).astype(bf16)
+            put(seq, slab).start()
+        return carry
+
+    lax.fori_loop(0, SEQS * HEADS // 2, one, 0)
+
+    def drain(step, carry):
+        put(lax.div(step, HEADS), lax.rem(step, HEADS)).wait()
+        return carry
+
+    lax.fori_loop(0, SEQS * HEADS, drain, 0)
 
 
 def body(queries_in, keys_in, values_in, gate_rows, out_weight):

time: 59.8 us -> 60.7 us (1.015)
  Pallas kernels: 59.5 us -> 60.6 us
    pallas_call x1, Pallas kernels: 44.5 us -> 50.3 us  [body(): pl.pallas_call(attention, out_shape=tuple((jax.ShapeDtypeStruct(*shape) f...]
    pallas_call x1, Pallas kernels: 15 us -> 10.3 us  [body(): pl.pallas_call(finish, out_shape=jax.ShapeDtypeStruct((SEQS, T, WIDTH), b...]
where the time goes in v6:
time: 60.7 us; the launch traced here: 60.6 us
  Pallas kernels  60.6 us (100%)
    pallas_call x1, Pallas kernels, body(): pl.pallas_call(attention, out_shape=tuple((jax.ShapeDtypeStruct(*shape) f...  50.3 us
    pallas_call x1, Pallas kernels, body(): pl.pallas_call(finish, out_shape=jax.ShapeDtypeStruct((SEQS, T, WIDTH), b...  10.3 us

profile of v6, /device:TPU:1, one launch (start us, length us, event | category | flops | bytes accessed | tf_op | source)
XLA Modules:
  0.0 60.6 jit_solution(5559975887966382588)
XLA Ops:
  0.0 50.3 %attention.1 = (f32[2,16,512,128]{3,2,1,0:T(8,128)}, bf16[2,6,512,128]{3,2,1,0:T(8,128)(2,1)}, bf16[6,2,2,32,2048]{4,3,2,1,0:T(8,128)(2,1)}) custom-call(bf16[2,512,16,128]{3,2,1,0:T(8,128)(2,1)} %q_in.1, bf16[2,512,16,128]{3,2,1,0:T(8,128)(2,1)} %k_in.1, bf16[2,512,16,128]{3,2,1,0:T(8,128)(2,1)} %v_in.1, bf16[2,512,16,128]{3,2,1,0:T(8,128)(2,1)} %g_in.1, ...), custom_call_target="tpu_custom_call" | custom-call | tf_op jit(solution)/shard_map/attention/pallas_call | solution.py:534
  50.3 10.3 %finish.1 = bf16[2,512,2048]{2,1,0:T(8,128)(2,1)} custom-call(f32[2,16,512,128]{3,2,1,0:T(8,128)} %get-tuple-element.8.sums, bf16[2,6,512,128]{3,2,1,0:T(8,128)(2,1)} %get-tuple-element.9.mixed, bf16[6,2,2,32,2048]{4,3,2,1,0:T(8,128)(2,1)} %get-tuple-element.10.weight), custom_call_target="tpu_custom_call" | custom-call | tf_op jit(solution)/shard_map/finish/pallas_call | solution.py:561

commit v7 on v4

--- a/solution.py
+++ b/solution.py
@@ -64,7 +64,7 @@
     for seq in range(SEQS):
         for group in range(2):
             c = 2 * seq + group
-            units.append((("last", c), 0.02, (("sum", 3, c),)))
+            units.append((("last", c), 0.02, (("sum", 4, c),)))
         for group in range(4):
             units.append((("read", seq, group), 0.3, (("last", 2 * seq), ("last", 2 * seq + 1))))
     for half in range(2):
@@ -94,14 +94,16 @@
             clock = ready[token]
         if token in ready:
             del ready[token]
-            clock += (0.25, 0.15, 0.15, 0.0)[token[1]] if token[0] == "sum" else 0.05
+            clock += (0.25, 0.15, 0.15, 0.02, 0.0)[token[1]] if token[0] == "sum" else 0.05
             if token in (("weight", 18), ("weight", 29)):
                 ready["here", int(token[1] == 29)] = clock + 1.6
             if token[0] == "sum" and token[1] < 3:
-                link = max(link, clock) + wire
+                link = max(link, clock) + wire / (1 if token[1] < 2 else 2)
                 ready["sum", token[1] + 1, token[2]] = link + hop
+            elif token[0] == "sum" and token[1] == 3:
+                ready["sum", 4, token[2]] = clock + 1.4
         done.add(token)
-        if token[:2] != ("sum", 3) and token[0] != "here":
+        if token[:2] != ("sum", 4) and token[0] != "here":
             plan.append(token)
     return plan
 
@@ -266,20 +268,24 @@
             device_id=(o, peers[side][stage]), device_id_type=MESH,
         )
 
-    def state_copy(c, side, to):
+    def quarter_copy(c, side):
         rows = pl.ds(base_row(c, 0) + quarter_row(side, True), quarter)
-        peer = peers[side][0]
         return pltpu.make_async_remote_copy(
             src_ref=state.at[rows], dst_ref=state.at[rows],
-            send_sem=st_send.at[c, side, to], recv_sem=st_recv.at[c, side, to],
-            device_id=(o, (peer, peer + 1 - 2 * core, other)[to]), device_id_type=MESH,
+            send_sem=z_send.at[c, 2, side], recv_sem=z_recv.at[c, 2, side],
+            device_id=(o, peers[side][0]), device_id_type=MESH,
+        )
+
+    def state_copy(c):
+        rows = pl.ds(base_row(c, 0), CROWS)
+        return pltpu.make_async_remote_copy(
+            src_ref=state.at[rows], dst_ref=state.at[rows],
+            send_sem=st_send.at[c], recv_sem=st_recv.at[c],
+            device_id=(o, other), device_id_type=MESH,
         )
 
     def take_state(c):
-        for side in range(2):
-            for to in range(3):
-                rows = pl.ds(base_row(c, int(to > 0)) + quarter_row(side, to == 2), quarter)
-                arrival(state.at[rows], st_recv.at[c, side, to])
+        arrival(state.at[pl.ds(base_row(c, 1), CROWS)], st_recv.at[c])
 
     def reduce(stage, c):
         if stage == 0:
@@ -288,6 +294,11 @@
             part[rows, :] = part[rows, :] + core_in[c]
             for side in range(2):
                 z_copy(c, 0, side).start()
+        elif stage == 3:
+            for side in range(2):
+                rows = pl.ds(base_row(c, 0) + quarter_row(side, False), quarter)
+                arrival(state.at[rows], z_recv.at[c, 2, side])
+            state_copy(c).start()
         else:
             for side in range(2):
                 z_copy(c, stage - 1, side).wait_recv()
@@ -298,8 +309,7 @@
                     z_copy(c, 1, side).start()
                 else:
                     state[rows, :] = total.astype(bf16)
-                    for to in range(3):
-                        state_copy(c, side, to).start()
+                    quarter_copy(c, side).start()
 
     def mass_copy(seq, d):
         return pltpu.make_async_remote_copy(
@@ -420,8 +430,8 @@
         for side in range(2):
             for stage in range(2):
                 z_copy(c, stage, side).wait_send()
-            for to in range(3):
-                state_copy(c, side, to).wait_send()
+            quarter_copy(c, side).wait_send()
+        state_copy(c).wait_send()
     for seq in range(SEQS):
         for slab in range(HEADS):
             out_copy(seq, slab).wait()
@@ -470,8 +480,8 @@
             pltpu.VMEM((SEQS, HEADS, T, D), bf16),
             pltpu.VMEM((16, 2, 2, ROWS, WIDTH), bf16),
             dma((4, SEQS, PIECES)), dma, dma((SEQS, HEADS)),
-            dma((CHUNKS,)), dma((CHUNKS,)), dma((CHUNKS, 2, 2)), dma((CHUNKS, 2, 2)),
-            dma((CHUNKS, 2, 3)), dma((CHUNKS, 2, 3)), dma((SEQS, 8)), dma((SEQS, 8)),
+            dma((CHUNKS,)), dma((CHUNKS,)), dma((CHUNKS, 3, 2)), dma((CHUNKS, 3, 2)),
+            dma((CHUNKS,)), dma((CHUNKS,)), dma((SEQS, 8)), dma((SEQS, 8)),
             dma((5, 4, 4, 2)), dma((4, 4, 2)), dma((4, 4, 2)),
         ],
         compiler_params=pltpu.CompilerParams(

time: 50.8 us -> 50 us (0.984)
  Pallas kernels: 50.6 us -> 49.8 us
    pallas_call x1, Pallas kernels: 46.7 us -> 45.9 us  [body(): pl.pallas_call(attention, out_shape=jax.ShapeDtypeStruct((SEQS, T, WIDTH)...]
where the time goes in v7:
time: 50 us; the launch traced here: 49.9 us
  Pallas kernels  49.8 us (100%)
    pallas_call x1, Pallas kernels, body(): pl.pallas_call(attention, out_shape=jax.ShapeDtypeStruct((SEQS, T, WIDTH)...  45.9 us
    pallas_call x1, Pallas kernels, body(): pl.pallas_call(hand_over, out_shape=jax.ShapeDtypeStruct((SEQS, T, WIDTH)...  3.85 us

profile of v7, /device:TPU:1, one launch (start us, length us, event | category | flops | bytes accessed | tf_op | source)
XLA Modules:
  0.0 49.9 jit_solution(18046033055185172445)
XLA Ops:
  0.0 45.9 %attention.1.src = bf16[2,512,2048]{2,1,0:T(8,128)(2,1)} custom-call(bf16[2,512,16,128]{3,2,1,0:T(8,128)(2,1)} %q_in.1, bf16[2,512,16,128]{3,2,1,0:T(8,128)(2,1)} %k_in.1, bf16[2,512,16,128]{3,2,1,0:T(8,128)(2,1)} %v_in.1, bf16[2,512,16,128]{3,2,1,0:T(8,128)(2,1)} %g_in.1, bf16[2,2,32,2048]{3,2,1,0:T(8,128)(2,1)} %bitcast.1), custom_call_target="tpu_custom_call" | custom-call | tf_op jit(solution)/shard_map/attention/pallas_call | solution.py:464
  45.9 3.9 %hand_over.1 = bf16[2,512,2048]{2,1,0:T(8,128)(2,1)} custom-call(bf16[2,512,2048]{2,1,0:T(8,128)(2,1)} %attention.1.src), custom_call_target="tpu_custom_call" | custom-call | tf_op jit(solution)/shard_map/hand_over/pallas_call | solution.py:492

commit v8 on v7

--- a/solution.py
+++ b/solution.py
@@ -42,7 +42,7 @@
 
 
 def make_plan():
-    begin, weights_at, wire, hop = 2.5, 2.4, 1.4, 3.4
+    begin, weights_at, wire, hop = 1.5, 1.5, 1.4, 3.4
     units = []
     for seq in range(SEQS):
         for half in range(2):
@@ -65,12 +65,12 @@
         for group in range(2):
             c = 2 * seq + group
             units.append((("last", c), 0.02, (("sum", 4, c),)))
-        for group in range(4):
-            units.append((("read", seq, group), 0.3, (("last", 2 * seq), ("last", 2 * seq + 1))))
+            for four in (group, group + 2):
+                units.append((("read", seq, four), 0.3, (("last", c),)))
     for half in range(2):
         for seq in range(SEQS):
             for quarter in range(4):
-                before = (("read", seq, 3),) if half == 0 else (("project", 0, seq, 3),)
+                before = tuple(("read", seq, four) for four in range(4)) if half == 0 else (("project", 0, seq, 3),)
                 units.append((("project", half, seq, quarter), (0.75, 0.48)[half], before + (("here", half),)))
 
     ready = {("weight", i): weights_at + at for i, at in enumerate(ARRIVE)}

time: 50 us -> 50.2 us (level)
  no operation moved by 1% of the time
where the time goes in v8:
time: 50.2 us; the launch traced here: 50.1 us
  Pallas kernels  49.9 us (99%)
    pallas_call x1, Pallas kernels, body(): pl.pallas_call(attention, out_shape=jax.ShapeDtypeStruct((SEQS, T, WIDTH)...  46.1 us
    pallas_call x1, Pallas kernels, body(): pl.pallas_call(hand_over, out_shape=jax.ShapeDtypeStruct((SEQS, T, WIDTH)...  3.85 us

profile of v8, /device:TPU:1, one launch (start us, length us, event | category | flops | bytes accessed | tf_op | source)
XLA Modules:
  0.0 50.1 jit_solution(13636092220949359603)
XLA Ops:
  0.0 46.1 %attention.1.src = bf16[2,512,2048]{2,1,0:T(8,128)(2,1)} custom-call(bf16[2,512,16,128]{3,2,1,0:T(8,128)(2,1)} %q_in.1, bf16[2,512,16,128]{3,2,1,0:T(8,128)(2,1)} %k_in.1, bf16[2,512,16,128]{3,2,1,0:T(8,128)(2,1)} %v_in.1, bf16[2,512,16,128]{3,2,1,0:T(8,128)(2,1)} %g_in.1, bf16[2,2,32,2048]{3,2,1,0:T(8,128)(2,1)} %bitcast.1), custom_call_target="tpu_custom_call" | custom-call | tf_op jit(solution)/shard_map/attention/pallas_call | solution.py:464
  46.1 3.9 %hand_over.1 = bf16[2,512,2048]{2,1,0:T(8,128)(2,1)} custom-call(bf16[2,512,2048]{2,1,0:T(8,128)(2,1)} %attention.1.src), custom_call_target="tpu_custom_call" | custom-call | tf_op jit(solution)/shard_map/hand_over/pallas_call | solution.py:492
